TPU v7x, 256 devices: a 8x8x2 block of a 8x8x16 slice. The times are simulated.
256 devices in a mesh: groups: 2 (over z), lat: 128 (over y, x, core).
Axes of the slice: x: 8, y: 8, z: 2, core: 2. Of those that a mesh axis runs over, the one named last changes fastest.
The devices are a block of a 8x8x16 slice.
Arguments:
- grid: bfloat16 [8192, 16, 8192], P('lat', 'groups'), parts along dimension 1, may hold values from -6 to 6
- cycle_weights: float32 [8192], P('lat'), may hold values from 0.1 to 1
- order_ids: int32 [38], replicated, may hold values from 0 to 4095, as said below
- leaf_weight: bfloat16 [8192, 38, 64], P('lat'), may hold values from -0.75 to 0.75
- transfer: bfloat16 [7, 128, 38, 64, 128], P(None, 'lat'), may hold values from -0.5 to 0.5
- degree_weight: bfloat16 [4096, 38, 64], P('lat'), may hold values from -0.75 to 0.75
Outputs:
- spectrum: float32 [4096, 38, 32], P('lat', None, 'groups'), parts along dimension 2
There are 2 independent parts, one for each index of `groups`. A program takes and returns all parts, laid end to end along the dimension named above; an argument that names none is the same for every part. Nothing has to cross between parts.
Inputs may be any that keep to these rules, and one draw needn't show every extreme that they name: `order_ids`: the 38 entries are distinct orders.
All inputs are finite; a program needn't handle non-finite values.
Results may differ from a plain program's by a relative error of at most 0.0023.
Values may be sent and summed in bfloat16 or wider, within the bound.
No kernel may reach another device: no remote copies, remote signals or barrier semaphores. Data moves between devices by JAX's collectives and lax.ppermute only.
A program may use at most 64 MiB of HBM per device.

v0:
```python
import math

import jax
import jax.numpy as jnp
from jax import lax
from jax.sharding import PartitionSpec as P


def from_partner(block, axis, distance):
    count = lax.axis_size(axis)
    route = []
    for low in range(count):
        high = low | 1 << distance
        if high != low and high < count:
            route += [(low, high), (high, low)]
    return lax.ppermute(block, axis, route)


def spectra(grid, cycle_weights, order_ids):
    cycles, fields, nlon = grid.shape
    count = order_ids.shape[0]
    longitude = lax.iota(jnp.int32, nlon)
    index = order_ids[:, None] * longitude[None, :] % nlon
    angle = index.astype(jnp.float32) * jnp.float32(2.0 * math.pi / nlon)
    table = jnp.concatenate([jnp.cos(angle), -jnp.sin(angle)], 0).astype(jnp.bfloat16)
    raw = lax.dot_general(
        grid.reshape(cycles * fields, nlon),
        table,
        (((1,), (1,)), ((), ())),
        preferred_element_type=jnp.float32,
    )
    raw = (
        raw.reshape(cycles, fields, 2, count)
        .transpose(0, 2, 1, 3)
        .reshape(cycles, 2 * fields, count)
    )
    return raw * (cycle_weights[:, None, None] / jnp.float32(math.sqrt(nlon)))


def combine(own, other, upper, factors):
    lower_half = jnp.where(upper, other, own)
    upper_half = jnp.where(upper, own, other)
    joined = jnp.concatenate([lower_half, upper_half], axis=1)
    return jnp.einsum(
        "ors,osq->orq", factors.astype(jnp.float32), joined, precision=lax.Precision.HIGHEST
    )


def single_level(current, factors, level, position):
    partner = from_partner(current, "lat", level)
    upper = position // 2**level % 2 == 1
    return combine(current, partner, upper, factors)


def body(grid, cycle_weights, order_ids, leaf_weight, transfer, degree_weight):
    waves = spectra(grid, cycle_weights, order_ids)
    current = jnp.einsum(
        "jor,jqo->orq", leaf_weight.astype(jnp.float32), waves, precision=lax.Precision.HIGHEST
    )
    position = lax.axis_index("lat")
    levels = transfer.shape[0]
    for level in range(levels):
        current = single_level(current, transfer[level, 0], level, position)
    per_node = degree_weight.shape[0]
    result = jnp.einsum(
        "dor,orq->doq", degree_weight.astype(jnp.float32), current, precision=lax.Precision.HIGHEST
    )
    degree = position * per_node + lax.iota(jnp.int32, per_node)
    keep = degree[:, None] >= order_ids[None, :]
    return jnp.where(keep[:, :, None], result, jnp.float32(0.0))


def solution(mesh):
    return jax.shard_map(
        body,
        mesh=mesh,
        in_specs=(
            P("lat", "groups", None),
            P("lat"),
            P(),
            P("lat", None, None),
            P(None, "lat", None, None, None),
            P("lat", None, None),
        ),
        out_specs=P("lat", None, "groups"),
        check_vma=False,
    )
```

profile of v0, /device:TPU:513, one launch (start us, length us, event | category | flops | bytes accessed | tf_op | source)
XLA Modules:
  0.0 135.9 jit_solution(14439627945594968816)
XLA Ops:
  0.0 0.0 copy-start
  0.0 6.4 %cosine_convert_fusion = (bf16[38,8192]{1,0:T(8,128)(2,1)S(1)}, bf16[38,8192]{1,0:T(8,128)(2,1)S(1)}) fusion(s32[38]{0:T(128)} %param.8), kind=kLoop, calls=%fused_computation.12 | loop fusion | flops 5292032 | bytes 1245336 | tf_op jit(solution)/shard_map/convert
  6.4 6.0 %fusion.12 = f32[512,76]{0,1:T(8,128)S(1)} fusion(bf16[64,8,8192]{2,1,0:T(8,128)(2,1)} %param.6, bf16[38,8192]{1,0:T(8,128)(2,1)S(1)} %get-tuple-element.20, bf16[38,8192]{1,0:T(8,128)(2,1)S(1)} %get-tuple-element.19), kind=kOutput, calls=%fused_computation.25 | convolution fusion | flops 640024576 | bytes 9789440 | tf_op jit(solution)/shard_map/dot_general | solution.py:26
  12.5 0.0 copy-start.3
  12.5 0.1 copy.11
  12.6 0.3 reshape.43
  12.9 0.4 copy.12
  13.3 0.0 copy-done.3
  13.4 0.0 copy-done
  13.4 0.6 convolution_bitcast_fusion.7
  14.0 20.5 %collective-permute-start = (f32[38,64,16]{1,2,0:T(8,128)S(1)}, f32[38,64,16]{1,2,0:T(8,128)S(1)}, u32[]{:S(2)}, u32[]{:S(2)}) collective-permute-start(f32[38,64,16]{1,2,0:T(8,128)S(1)} %convolution_bitcast_fusion.7), channel_id=1, source_target_pairs={{0,1},{1,0},{2,3},{3,2},{4,5},{5,4},{6,7},{7,6},{8,9},{9,8},{10,11... | collective-permute-start | bytes 466952 | tf_op jit(solution)/shard_map/ppermute | solution.py:16
  34.5 1.2 collective-permute-done
  35.8 2.2 %convolution_bitcast_fusion.6 = f32[38,64,16]{1,2,0:T(8,128)S(1)} fusion(bf16[7,1,38,64,128]{4,3,2,1,0:T(8,128)(2,1)} %param.10, f32[38,64,16]{1,2,0:T(8,128)S(1)} %get-tuple-element.18, f32[38,64,16]{1,2,0:T(8,128)S(1)} %get-tuple-element.17), kind=kOutput, calls=%fused_computation.23 | convolution fusion | flops 59846656 | bytes 1089536 | tf_op jit(solution)/shard_map/ors,osq->orq/dot_general | solution.py:44
  38.0 0.1 collective-permute-start.1
  38.2 8.5 %collective-permute-done.1 = f32[38,64,16]{1,2,0:T(8,128)S(1)} collective-permute-done((f32[38,64,16]{1,2,0:T(8,128)S(1)}, f32[38,64,16]{1,2,0:T(8,128)S(1)}, u32[]{:S(2)}, u32[]{:S(2)}) %collective-permute-start.1) | collective-permute-done | bytes 155680 | tf_op jit(solution)/shard_map/ppermute | solution.py:16
  46.7 2.2 %convolution_bitcast_fusion.5 = f32[38,64,16]{1,2,0:T(8,128)S(1)} fusion(bf16[7,1,38,64,128]{4,3,2,1,0:T(8,128)(2,1)} %param.10, f32[38,64,16]{1,2,0:T(8,128)S(1)} %get-tuple-element.16, f32[38,64,16]{1,2,0:T(8,128)S(1)} %get-tuple-element.15), kind=kOutput, calls=%fused_computation.22 | convolution fusion | flops 59846656 | bytes 1089536 | tf_op jit(solution)/shard_map/ors,osq->orq/dot_general | solution.py:44
  48.9 0.1 collective-permute-start.2
  49.1 16.8 %collective-permute-done.2 = f32[38,64,16]{1,2,0:T(8,128)S(1)} collective-permute-done((f32[38,64,16]{1,2,0:T(8,128)S(1)}, f32[38,64,16]{1,2,0:T(8,128)S(1)}, u32[]{:S(2)}, u32[]{:S(2)}) %collective-permute-start.2) | collective-permute-done | bytes 155680 | tf_op jit(solution)/shard_map/ppermute | solution.py:16
  65.9 2.2 %convolution_bitcast_fusion.4 = f32[38,64,16]{1,2,0:T(8,128)S(1)} fusion(bf16[7,1,38,64,128]{4,3,2,1,0:T(8,128)(2,1)} %param.10, f32[38,64,16]{1,2,0:T(8,128)S(1)} %get-tuple-element.14, f32[38,64,16]{1,2,0:T(8,128)S(1)} %get-tuple-element.13), kind=kOutput, calls=%fused_computation.21 | convolution fusion | flops 59846656 | bytes 1089536 | tf_op jit(solution)/shard_map/ors,osq->orq/dot_general | solution.py:44
  68.1 0.1 collective-permute-start.3
  68.3 16.1 %collective-permute-done.3 = f32[38,64,16]{1,2,0:T(8,128)S(1)} collective-permute-done((f32[38,64,16]{1,2,0:T(8,128)S(1)}, f32[38,64,16]{1,2,0:T(8,128)S(1)}, u32[]{:S(2)}, u32[]{:S(2)}) %collective-permute-start.3) | collective-permute-done | bytes 155680 | tf_op jit(solution)/shard_map/ppermute | solution.py:16
  84.4 2.2 %convolution_bitcast_fusion.3 = f32[38,64,16]{1,2,0:T(8,128)S(1)} fusion(bf16[7,1,38,64,128]{4,3,2,1,0:T(8,128)(2,1)} %param.10, f32[38,64,16]{1,2,0:T(8,128)S(1)} %get-tuple-element.12, f32[38,64,16]{1,2,0:T(8,128)S(1)} %get-tuple-element.11), kind=kOutput, calls=%fused_computation.20 | convolution fusion | flops 59846656 | bytes 1089536 | tf_op jit(solution)/shard_map/ors,osq->orq/dot_general | solution.py:44
  86.6 0.1 collective-permute-start.4
  86.8 7.4 %collective-permute-done.4 = f32[38,64,16]{1,2,0:T(8,128)S(1)} collective-permute-done((f32[38,64,16]{1,2,0:T(8,128)S(1)}, f32[38,64,16]{1,2,0:T(8,128)S(1)}, u32[]{:S(2)}, u32[]{:S(2)}) %collective-permute-start.4) | collective-permute-done | bytes 155680 | tf_op jit(solution)/shard_map/ppermute | solution.py:16
  94.2 2.2 %convolution_bitcast_fusion.2 = f32[38,64,16]{1,2,0:T(8,128)S(1)} fusion(bf16[7,1,38,64,128]{4,3,2,1,0:T(8,128)(2,1)} %param.10, f32[38,64,16]{1,2,0:T(8,128)S(1)} %get-tuple-element.10, f32[38,64,16]{1,2,0:T(8,128)S(1)} %get-tuple-element.9), kind=kOutput, calls=%fused_computation.19 | convolution fusion | flops 59846656 | bytes 1089536 | tf_op jit(solution)/shard_map/ors,osq->orq/dot_general | solution.py:44
  96.4 0.3 collective-permute-start.5
  96.8 0.0 copy-start.2
  96.8 16.7 %collective-permute-done.5 = f32[38,64,16]{1,2,0:T(8,128)S(1)} collective-permute-done((f32[38,64,16]{1,2,0:T(8,128)S(1)}, f32[38,64,16]{1,2,0:T(8,128)S(1)}, u32[]{:S(2)}, u32[]{:S(2)}) %collective-permute-start.5) | collective-permute-done | bytes 155680 | tf_op jit(solution)/shard_map/ppermute | solution.py:16
  113.6 2.2 %convolution_bitcast_fusion.1 = f32[38,64,16]{1,2,0:T(8,128)S(1)} fusion(bf16[7,1,38,64,128]{4,3,2,1,0:T(8,128)(2,1)} %param.10, f32[38,64,16]{1,2,0:T(8,128)S(1)} %get-tuple-element.8, f32[38,64,16]{1,2,0:T(8,128)S(1)} %get-tuple-element.7), kind=kOutput, calls=%fused_computation.18 | convolution fusion | flops 59846656 | bytes 1089536 | tf_op jit(solution)/shard_map/ors,osq->orq/dot_general | solution.py:44
  115.8 0.1 collective-permute-start.6
  116.0 0.0 copy-done.2
  116.0 0.1 broadcast_compare_fusion
  116.0 0.0 copy-start.1
  116.1 16.0 %collective-permute-done.6 = f32[38,64,16]{1,2,0:T(8,128)S(1)} collective-permute-done((f32[38,64,16]{1,2,0:T(8,128)S(1)}, f32[38,64,16]{1,2,0:T(8,128)S(1)}, u32[]{:S(2)}, u32[]{:S(2)}) %collective-permute-start.6) | collective-permute-done | bytes 155680 | tf_op jit(solution)/shard_map/ppermute | solution.py:16
  132.1 2.2 %fusion.17 = f32[38,16,64]{2,1,0:T(8,128)S(1)} fusion(bf16[7,1,38,64,128]{4,3,2,1,0:T(8,128)(2,1)} %param.10, f32[38,64,16]{1,2,0:T(8,128)S(1)} %get-tuple-element.6, f32[38,64,16]{1,2,0:T(8,128)S(1)} %get-tuple-element.5), kind=kOutput, calls=%fused_computation.26 | convolution fusion | flops 59846656 | bytes 1089536 | tf_op jit(solution)/shard_map/ors,osq->orq/dot_general | solution.py:44
  134.3 0.0 copy-done.1
  134.3 0.6 fusion.11
  134.9 0.9 copy.13
  (9 shorter events, 0.3 us)
Async XLA Ops:
  0.0 13.4 %copy-start = (bf16[64,38,64]{2,0,1:T(8,128)(2,1)S(1)}, bf16[64,38,64]{2,0,1:T(8,128)(2,1)}, u32[]{:S(2)}) copy-start(bf16[64,38,64]{2,0,1:T(8,128)(2,1)} %param.9) | copy-start | bytes 933892
  12.5 0.9 copy-start.3
  14.0 21.8 %collective-permute-start = (f32[38,64,16]{1,2,0:T(8,128)S(1)}, f32[38,64,16]{1,2,0:T(8,128)S(1)}, u32[]{:S(2)}, u32[]{:S(2)}) collective-permute-start(f32[38,64,16]{1,2,0:T(8,128)S(1)} %convolution_bitcast_fusion.7), channel_id=1, source_target_pairs={{0,1},{1,0},{2,3},{3,2},{4,5},{5,4},{6,7},{7,6},{8,9},{9,8},{10,11... | collective-permute-start | bytes 466952 | tf_op jit(solution)/shard_map/ppermute | solution.py:16
  38.0 8.7 %collective-permute-start.1 = (f32[38,64,16]{1,2,0:T(8,128)S(1)}, f32[38,64,16]{1,2,0:T(8,128)S(1)}, u32[]{:S(2)}, u32[]{:S(2)}) collective-permute-start(f32[38,64,16]{1,2,0:T(8,128)S(1)} %convolution_bitcast_fusion.6), channel_id=1, source_target_pairs={{0,2},{2,0},{1,3},{3,1},{4,6},{6,4},{5,7},{7,5},{8,10},{10,8},{9,1... | collective-permute-start | bytes 466952 | tf_op jit(solution)/shard_map/ppermute | solution.py:16
  48.9 17.0 %collective-permute-start.2 = (f32[38,64,16]{1,2,0:T(8,128)S(1)}, f32[38,64,16]{1,2,0:T(8,128)S(1)}, u32[]{:S(2)}, u32[]{:S(2)}) collective-permute-start(f32[38,64,16]{1,2,0:T(8,128)S(1)} %convolution_bitcast_fusion.5), channel_id=1, source_target_pairs={{0,4},{4,0},{1,5},{5,1},{2,6},{6,2},{3,7},{7,3},{8,12},{12,8},{9,1... | collective-permute-start | bytes 466952 | tf_op jit(solution)/shard_map/ppermute | solution.py:16
  68.1 16.2 %collective-permute-start.3 = (f32[38,64,16]{1,2,0:T(8,128)S(1)}, f32[38,64,16]{1,2,0:T(8,128)S(1)}, u32[]{:S(2)}, u32[]{:S(2)}) collective-permute-start(f32[38,64,16]{1,2,0:T(8,128)S(1)} %convolution_bitcast_fusion.4), channel_id=1, source_target_pairs={{0,8},{8,0},{1,9},{9,1},{2,10},{10,2},{3,11},{11,3},{4,12},{12,4},... | collective-permute-start | bytes 466952 | tf_op jit(solution)/shard_map/ppermute | solution.py:16
  86.6 7.5 %collective-permute-start.4 = (f32[38,64,16]{1,2,0:T(8,128)S(1)}, f32[38,64,16]{1,2,0:T(8,128)S(1)}, u32[]{:S(2)}, u32[]{:S(2)}) collective-permute-start(f32[38,64,16]{1,2,0:T(8,128)S(1)} %convolution_bitcast_fusion.3), channel_id=1, source_target_pairs={{0,16},{16,0},{1,17},{17,1},{2,18},{18,2},{3,19},{19,3},{4,20},{20... | collective-permute-start | bytes 466952 | tf_op jit(solution)/shard_map/ppermute | solution.py:16
  96.4 17.1 %collective-permute-start.5 = (f32[38,64,16]{1,2,0:T(8,128)S(1)}, f32[38,64,16]{1,2,0:T(8,128)S(1)}, u32[]{:S(2)}, u32[]{:S(2)}) collective-permute-start(f32[38,64,16]{1,2,0:T(8,128)S(1)} %convolution_bitcast_fusion.2), channel_id=1, source_target_pairs={{0,32},{32,0},{1,33},{33,1},{2,34},{34,2},{3,35},{35,3},{4,36},{36... | collective-permute-start | bytes 466952 | tf_op jit(solution)/shard_map/ppermute | solution.py:16
  96.8 19.2 %copy-start.2 = (s32[38]{0:T(128)S(1)}, s32[38]{0:T(128)}, u32[]{:S(2)}) copy-start(s32[38]{0:T(128)} %param.8) | copy-start | bytes 460
  115.8 16.2 %collective-permute-start.6 = (f32[38,64,16]{1,2,0:T(8,128)S(1)}, f32[38,64,16]{1,2,0:T(8,128)S(1)}, u32[]{:S(2)}, u32[]{:S(2)}) collective-permute-start(f32[38,64,16]{1,2,0:T(8,128)S(1)} %convolution_bitcast_fusion.1), channel_id=1, source_target_pairs={{0,64},{64,0},{1,65},{65,1},{2,66},{66,2},{3,67},{67,3},{4,68},{68... | collective-permute-start | bytes 466952 | tf_op jit(solution)/shard_map/ppermute | solution.py:16
  116.0 18.3 %copy-start.1 = (bf16[32,38,64]{2,0,1:T(8,128)(2,1)S(1)}, bf16[32,38,64]{2,0,1:T(8,128)(2,1)}, u32[]{:S(2)}) copy-start(bf16[32,38,64]{2,0,1:T(8,128)(2,1)} %param.11) | copy-start | bytes 466948
where the time goes:
time: 136 us
  waiting for transfers between devices  82.7 us (61%)
  matrix products  22.7 us (17%)
  starting transfers between devices  21.6 us (16%)
  other arithmetic  6.8 us (5%)
  local copies, waits for them, and re-layouts  1.79 us (1%)
    ppermute x7, waiting for transfers between devices, from_partner(): return lax.ppermute(block, axis, route)  82.7 us
    ppermute x7, starting transfers between devices, from_partner(): return lax.ppermute(block, axis, route)  21.6 us
    dot_general x7, matrix products, combine(): jnp.einsum('ors,osq->orq', factors.astype(jnp.float32), joined, precision...  15.5 us
    another operation x1, other arithmetic  6.41 us
    dot_general x1, matrix products, spectra(): lax.dot_general(grid.reshape(cycles * fields, nlon), table, (((1,), (1,))...  6.05 us
  transfers between devices with their start and end apart: 7, of which 7 were waited for; matrix products, arithmetic and copies ran while one was open for 0% of the time, Pallas kernels for 0%

commit v1 on v0

v1 whole, which is shorter than its diff:
```python
import math

import jax
import jax.numpy as jnp
from jax import lax
from jax.experimental import pallas as pl
from jax.experimental.pallas import tpu as pltpu
from jax.sharding import PartitionSpec as P

F32, BF16, I16, I32 = jnp.float32, jnp.bfloat16, jnp.int16, jnp.int32
LANES = 128
BLOCK = 8
CODE = 32000.0


def from_partner(block, axis, distance):
    count = lax.axis_size(axis)
    route = []
    for low in range(count):
        high = low | 1 << distance
        if high != low and high < count:
            route += [(low, high), (high, low)]
    return lax.ppermute(block, axis, route)


def lanes_of(shape):
    return lax.broadcasted_iota(I32, shape, len(shape) - 1)


def cos_sin(step, nlon):
    quarter, eighth = nlon // 4, nlon // 8
    moved = step + eighth
    quadrant = moved // quarter & 3
    x = ((moved & quarter - 1) - eighth).astype(F32) * F32(2.0 * math.pi / nlon)
    y = x * x
    c = 1.0 + y * (-0.5 + y * (1 / 24 + y * (-1 / 720 + y * (1 / 40320 - y / 3628800))))
    s = x * (1.0 + y * (-1 / 6 + y * (1 / 120 + y * (-1 / 5040 + y / 362880))))
    swap = quadrant & 1 == 1
    cos = jnp.where(swap, s, c)
    sin = jnp.where(swap, c, s)
    cos = jnp.where((quadrant == 1) | (quadrant == 2), -cos, cos)
    sin = jnp.where(quadrant >= 2, -sin, sin)
    return cos, sin


def split(value):
    high = value.astype(BF16)
    return high, (value - high.astype(F32)).astype(BF16)


def encode(values, send):
    rank = values[0].shape[0]
    peak = jnp.full((8, LANES), 1e-30, F32)
    for value in values:
        for row in range(0, rank, 8):
            peak = jnp.maximum(peak, jnp.abs(value[row : row + 8]))
    exponent = jnp.ceil(jnp.log2(peak))
    scale = jnp.exp2(-exponent) * CODE
    scale = jnp.concatenate([scale] * (rank // 8), 0)
    for g, value in enumerate(values):
        send[g * rank : (g + 1) * rank, :] = (value * scale).astype(I32).astype(I16)
    both = jnp.concatenate([exponent, exponent], 0)
    send[len(values) * rank :, :] = both.astype(I32).astype(I16)


def pick(product, rows):
    lane = lanes_of((rows, LANES)) % BLOCK
    chosen = jnp.zeros((rows, LANES), F32)
    for o in range(product.shape[0] // rows):
        chosen = jnp.where(lane == o, product[o * rows : (o + 1) * rows], chosen)
    return chosen


def analyse_kernel(ids_hbm, weights_hbm, leaf_hbm, grid_hbm, own_ref, send_ref,
                   ids, weights, leaf, grid, table, turned, raw, sems, grid_sems, *, fields, pieces):
    rows, nlon = grid.shape
    orders, cycles, rank = leaf.shape
    piece = nlon // pieces
    groups = pl.cdiv(orders, BLOCK)
    loads = []
    for i in range(pieces):
        cut = (slice(None), slice(i * piece, (i + 1) * piece))
        loads.append(pltpu.make_async_copy(grid_hbm.at[cut], grid.at[cut], grid_sems.at[i]))
    ids_load = pltpu.make_async_copy(ids_hbm, ids, sems.at[0])
    weights_load = pltpu.make_async_copy(weights_hbm, weights, sems.at[1])
    leaf_load = pltpu.make_async_copy(leaf_hbm, leaf, sems.at[2])
    ids_load.start()
    loads[0].start()
    loads[1].start()
    weights_load.start()
    leaf_load.start()
    for load in loads[2:]:
        load.start()
    half = 48
    ids_load.wait()
    row = lax.broadcasted_iota(I32, (half, LANES), 0)
    order = jnp.zeros((half, LANES), I32)
    for o in range(orders):
        order = jnp.where(row == o, ids[o], order)
    fine_c, fine_s = cos_sin(order * lanes_of((half, LANES)) & nlon - 1, nlon)
    coarse_c, coarse_s = cos_sin(order * (lanes_of((half, LANES)) * LANES) & nlon - 1, nlon)
    turn_c = coarse_c[:, piece // LANES : piece // LANES + 1] + jnp.zeros((half, LANES), F32)
    turn_s = coarse_s[:, piece // LANES : piece // LANES + 1] + jnp.zeros((half, LANES), F32)
    for a in range(piece // LANES):
        ca, sa = coarse_c[:, a : a + 1], coarse_s[:, a : a + 1]
        c, s = ca * fine_c - sa * fine_s, sa * fine_c + ca * fine_s
        for i in range(pieces):
            at = slice(i * piece + a * LANES, i * piece + (a + 1) * LANES)
            table[0:half, at] = c.astype(BF16)
            table[64 : 64 + half, at] = (-s).astype(BF16)
            if i + 1 < pieces:
                c, s = c * turn_c - s * turn_s, s * turn_c + c * turn_s
    weights_load.wait()
    leaf_load.wait()
    for o in range(orders):
        turned[o * rank : (o + 1) * rank, :] = jnp.concatenate([leaf[o], leaf[o]], 0).T
    weight = jnp.broadcast_to(weights[:, :], (LANES, cycles)).T * F32(1.0 / math.sqrt(nlon))
    for i in range(pieces):
        loads[i].wait()
        at = slice(i * piece, (i + 1) * piece)
        part = lax.dot_general(grid[:, at], table[:, at], (((1,), (1,)), ((), ())), preferred_element_type=F32)
        raw[:, :] = part if i == 0 else raw[:, :] + part
    moved = []
    for f in range(fields):
        value = raw[pl.ds(f, cycles, stride=fields), :] * weight
        moved.append(pltpu.roll(value, BLOCK * f, 1) if f else value)
    slot = lanes_of((cycles, LANES)) // BLOCK
    results = []
    for g in range(groups):
        here = slot - g & fields - 1
        waves = moved[0]
        for f in range(1, fields):
            waves = jnp.where(here == f, moved[f], waves)
        high, low = split(waves)
        count = min(BLOCK, orders - g * BLOCK)
        at = slice(g * BLOCK * rank, (g * BLOCK + count) * rank)
        product = jnp.dot(turned[at, :], jnp.concatenate([high, low], 0), preferred_element_type=F32)
        results.append(pick(product, rank))
    for g in range(groups):
        own_ref[g * rank : (g + 1) * rank, :] = results[g]
    encode(results, send_ref)


def join(own_ref, got_ref, joined, upper, groups, rank):
    exponent = got_ref[groups * rank :, :].astype(I32).astype(F32)[0:8]
    scale = jnp.exp2(exponent) * F32(1.0 / CODE)
    scale = jnp.concatenate([scale] * (rank // 8), 0)
    for g in range(groups):
        at = slice(g * rank, (g + 1) * rank)
        own = own_ref[at, :]
        other = got_ref[at, :].astype(I32).astype(F32) * scale
        lower_half = jnp.where(upper, other, own)
        upper_half = jnp.where(upper, own, other)
        low_high, low_low = split(lower_half)
        up_high, up_low = split(upper_half)
        joined[g, 0:rank, :] = low_high
        joined[g, rank : 2 * rank, :] = up_high
        joined[g, 2 * rank : 3 * rank, :] = low_low
        joined[g, 3 * rank : 4 * rank, :] = up_low


def merge(factors, joined, groups):
    orders, rank, wide = factors.shape
    results = []
    for g in range(groups):
        count = min(BLOCK, orders - g * BLOCK)
        left = factors[g * BLOCK : g * BLOCK + count].reshape(count * rank, wide)
        product = jnp.dot(jnp.concatenate([left, left], 1), joined[g], preferred_element_type=F32)
        results.append(pick(product, rank))
    return results


def level_kernel(own_ref, got_ref, factors, next_ref, send_ref, joined, *, level):
    orders, rank, _ = factors.shape
    groups = joined.shape[0]
    upper = (lax.axis_index("lat") >> level) & 1 == 1
    join(own_ref, got_ref, joined, upper, groups, rank)
    results = merge(factors, joined, groups)
    for g in range(groups):
        next_ref[g * rank : (g + 1) * rank, :] = results[g]
    encode(results, send_ref)


def last_kernel(ids, own_ref, got_ref, factors, degree_weight, out_ref, joined, *, level):
    orders, rank, _ = factors.shape
    groups = joined.shape[0]
    degrees = degree_weight.shape[1]
    slots = LANES // BLOCK
    position = lax.axis_index("lat")
    upper = (position >> level) & 1 == 1
    join(own_ref, got_ref, joined, upper, groups, rank)
    finals = merge(factors, joined, groups)
    lane = lanes_of((degrees, LANES))
    degree = position * degrees + lax.broadcasted_iota(I32, (degrees, LANES), 0)
    outs = []
    for g in range(groups):
        count = min(BLOCK, orders - g * BLOCK)
        left = degree_weight[g * BLOCK : g * BLOCK + count].reshape(count * degrees, rank)
        high, low = split(finals[g])
        product = jnp.dot(left, jnp.concatenate([high, low], 1), preferred_element_type=F32)
        value = pick(product[:, :LANES] + product[:, LANES:], degrees)
        order = jnp.zeros((degrees, LANES), I32)
        for o in range(count):
            order = jnp.where(lane % BLOCK == o, ids[g * BLOCK + o], order)
        outs.append(jnp.where(degree >= order, value, F32(0.0)))
    slot = lane // BLOCK
    for q in range(slots):
        value = outs[0]
        for g in range(1, groups):
            value = jnp.where(slot == (q + g) % slots, outs[g], value)
        value = pltpu.roll(value, (LANES - BLOCK * q) % LANES, 1) if q else value
        out_ref[pl.ds(q, degrees, stride=slots), :] = value[:, :orders]


def body(grid, cycle_weights, order_ids, leaf_weight, transfer, degree_weight):
    cycles, fields, nlon = grid.shape
    orders, rank = leaf_weight.shape[1:]
    levels = transfer.shape[0]
    degrees = degree_weight.shape[0]
    groups = -(-orders // BLOCK)
    pieces = 8
    leaf = leaf_weight.transpose(1, 0, 2)
    last = degree_weight.transpose(1, 0, 2)
    hbm = pl.BlockSpec(memory_space=pl.ANY)
    vmem = pl.BlockSpec(memory_space=pltpu.VMEM)
    smem = pl.BlockSpec(memory_space=pltpu.SMEM)
    own_type = jax.ShapeDtypeStruct((groups * rank, LANES), F32)
    send_type = jax.ShapeDtypeStruct((groups * rank + 16, LANES), I16)
    joined = pltpu.VMEM((groups, 4 * rank, LANES), BF16)
    own, send = pl.pallas_call(
        lambda *refs: analyse_kernel(*refs, fields=fields, pieces=pieces),
        out_shape=(own_type, send_type),
        in_specs=[hbm] * 4,
        out_specs=(vmem, vmem),
        scratch_shapes=[
            pltpu.SMEM((orders,), I32),
            pltpu.VMEM((1, cycles), F32),
            pltpu.VMEM((orders, cycles, rank), BF16),
            pltpu.VMEM((cycles * fields, nlon), BF16),
            pltpu.VMEM((LANES, nlon), BF16),
            pltpu.VMEM((orders * rank, 2 * cycles), BF16),
            pltpu.VMEM((cycles * fields, LANES), F32),
            pltpu.SemaphoreType.DMA((3,)),
            pltpu.SemaphoreType.DMA((pieces,)),
        ],
        name="analyse",
    )(order_ids, cycle_weights.reshape(1, cycles), leaf, grid.reshape(cycles * fields, nlon))
    for level in range(levels):
        got = from_partner(send, "lat", level)
        factors = transfer[level, 0]
        if level + 1 < levels:
            own, send = pl.pallas_call(
                lambda *refs, level=level: level_kernel(*refs, level=level),
                out_shape=(own_type, send_type),
                in_specs=[vmem, vmem, vmem],
                out_specs=(vmem, vmem),
                scratch_shapes=[joined],
                name=f"level{level}",
            )(own, got, factors)
        else:
            out = pl.pallas_call(
                lambda *refs: last_kernel(*refs, level=level),
                out_shape=jax.ShapeDtypeStruct((degrees * 2 * fields, orders), F32),
                in_specs=[smem, vmem, vmem, vmem, vmem],
                out_specs=vmem,
                scratch_shapes=[joined],
                name="last",
            )(order_ids, own, got, factors, last)
    return out.reshape(degrees, 2 * fields, orders).transpose(0, 2, 1)


def solution(mesh):
    return jax.shard_map(
        body,
        mesh=mesh,
        in_specs=(
            P("lat", "groups", None),
            P("lat"),
            P(),
            P("lat", None, None),
            P(None, "lat", None, None, None),
            P("lat", None, None),
        ),
        out_specs=P("lat", None, "groups"),
        check_vma=False,
    )
```

time: 136 us -> 93.5 us (0.69)
  the two profiles are of different devices: /device:TPU:513 before, /device:TPU:528 now
where the time goes in v1:
time: 93.5 us; the launch traced here: 92.2 us
  waiting for transfers between devices  28.3 us (30%)
  starting transfers between devices  28.2 us (30%)
  Pallas kernels  26.9 us (29%)
  local copies, waits for them, and re-layouts  8.73 us (9%)
    ppermute x7, waiting for transfers between devices, from_partner(): return lax.ppermute(block, axis, route)  28.3 us
    ppermute x7, starting transfers between devices, from_partner(): return lax.ppermute(block, axis, route)  28.2 us
    pallas_call x6, Pallas kernels, body(): pl.pallas_call(lambda *refs, level=level: level_kernel(*refs, level=level...  14.6 us
    pallas_call x1, Pallas kernels, body(): pl.pallas_call(lambda *refs: analyse_kernel(*refs, fields=fields, pieces=...  9.48 us
    unnamed x14, local copies, waits for them, and re-layouts  4.4 us
    squeeze x1, local copies, waits for them, and re-layouts, body(): factors = transfer[level, 0]  4.32 us
    pallas_call x1, Pallas kernels, body(): pl.pallas_call(lambda *refs: last_kernel(*refs, level=level), out_shape=j...  2.87 us
  transfers between devices with their start and end apart: 7, of which 6 were waited for; matrix products, arithmetic and copies ran while one was open for 5% of the time, Pallas kernels for 0%

profile of v1, /device:TPU:528, one launch (start us, length us, event | category | flops | bytes accessed | tf_op | source)
XLA Modules:
  0.0 92.2 jit_solution(7761027203708782141)
XLA Ops:
  0.0 9.5 %analyse.1 = (f32[320,128]{1,0:T(8,128)}, s16[336,128]{1,0:T(8,128)(2,1)}) custom-call(s32[38]{0:T(128)} %refs_0_.3, f32[1,64]{1,0:T(1,128)} %bitcast.24, bf16[38,64,64]{2,1,0:T(8,128)(2,1)} %bitcast.22, bf16[512,8192]{1,0:T(8,128)(2,1)} %bitcast.21), custom_call_target="tpu_custom_call" | custom-call | tf_op jit(solution)/shard_map/analyse/pallas_call | solution.py:230
  9.5 0.1 collective-permute-start
  9.6 4.3 %slice_bitcast_fusion = (bf16[38,64,128]{2,1,0:T(8,128)(2,1)}, bf16[38,64,128]{2,1,0:T(8,128)(2,1)}, bf16[38,64,128]{2,1,0:T(8,128)(2,1)}, bf16[38,64,128]{2,1,0...) fusion(bf16[7,1,38,64,128]{4,3,2,1,0:T(8,128)(2,1)} %param.10), kind=kLoop, calls=%fused_computation | loop fusion | bytes 8716288 | tf_op jit(solution)/shard_map/squeeze | solution.py:250
  14.0 0.0 collective-permute-done.refs_1_
  14.0 0.0 copy-start
  14.0 0.6 copy-done
  14.6 2.4 %level0.1 = (f32[320,128]{1,0:T(8,128)}, s16[336,128]{1,0:T(8,128)(2,1)}) custom-call(f32[320,128]{1,0:T(8,128)} %get-tuple-element.19.refs_0_, s16[336,128]{1,0:T(8,128)(2,1)} %copy-done, bf16[38,64,128]{2,1,0:T(8,128)(2,1)} %get-tuple-element.38.refs_2_), custom_call_target="tpu_custom_call" | custom-call | tf_op jit(solution)/shard_map/level0/pallas_call | solution.py:252
  17.0 1.6 %collective-permute-start.1 = (s16[336,128]{1,0:T(8,128)(2,1)}, s16[336,128]{1,0:T(8,128)(2,1)S(1)}, u32[]{:S(2)}, u32[]{:S(2)}) collective-permute-start(s16[336,128]{1,0:T(8,128)(2,1)} %get-tuple-element.22), channel_id=1, source_target_pairs={{0,2},{2,0},{1,3},{3,1},{4,6},{6,4},{5,7},{7,5},{8,10},{10,8},{9,1... | collective-permute-start | bytes 258056 | tf_op jit(solution)/shard_map/ppermute | solution.py:23
  18.7 3.5 %collective-permute-done.1.refs_1_ = s16[336,128]{1,0:T(8,128)(2,1)S(1)} collective-permute-done((s16[336,128]{1,0:T(8,128)(2,1)}, s16[336,128]{1,0:T(8,128)(2,1)S(1)}, u32[]{:S(2)}, u32[]{:S(2)}) %collective-permute-start.1) | collective-permute-done | bytes 86048 | tf_op jit(solution)/shard_map/ppermute | solution.py:23
  22.2 0.0 copy-start.1
  22.2 0.6 copy-done.1
  22.8 2.4 %level1.1 = (f32[320,128]{1,0:T(8,128)}, s16[336,128]{1,0:T(8,128)(2,1)}) custom-call(f32[320,128]{1,0:T(8,128)} %get-tuple-element.21.refs_0_, s16[336,128]{1,0:T(8,128)(2,1)} %copy-done.1, bf16[38,64,128]{2,1,0:T(8,128)(2,1)} %get-tuple-element.37.refs_2_), custom_call_target="tpu_custom_call" | custom-call | tf_op jit(solution)/shard_map/level1/pallas_call | solution.py:252
  25.2 2.7 %collective-permute-start.2 = (s16[336,128]{1,0:T(8,128)(2,1)}, s16[336,128]{1,0:T(8,128)(2,1)S(1)}, u32[]{:S(2)}, u32[]{:S(2)}) collective-permute-start(s16[336,128]{1,0:T(8,128)(2,1)} %get-tuple-element.24), channel_id=1, source_target_pairs={{0,4},{4,0},{1,5},{5,1},{2,6},{6,2},{3,7},{7,3},{8,12},{12,8},{9,1... | collective-permute-start | bytes 258056 | tf_op jit(solution)/shard_map/ppermute | solution.py:23
  27.9 4.5 %collective-permute-done.2.refs_1_ = s16[336,128]{1,0:T(8,128)(2,1)S(1)} collective-permute-done((s16[336,128]{1,0:T(8,128)(2,1)}, s16[336,128]{1,0:T(8,128)(2,1)S(1)}, u32[]{:S(2)}, u32[]{:S(2)}) %collective-permute-start.2) | collective-permute-done | bytes 86048 | tf_op jit(solution)/shard_map/ppermute | solution.py:23
  32.4 0.0 copy-start.2
  32.4 0.6 copy-done.2
  33.0 2.4 %level2.1 = (f32[320,128]{1,0:T(8,128)}, s16[336,128]{1,0:T(8,128)(2,1)}) custom-call(f32[320,128]{1,0:T(8,128)} %get-tuple-element.23.refs_0_, s16[336,128]{1,0:T(8,128)(2,1)} %copy-done.2, bf16[38,64,128]{2,1,0:T(8,128)(2,1)} %get-tuple-element.36.refs_2_), custom_call_target="tpu_custom_call" | custom-call | tf_op jit(solution)/shard_map/level2/pallas_call | solution.py:252
  35.5 5.8 %collective-permute-start.3 = (s16[336,128]{1,0:T(8,128)(2,1)}, s16[336,128]{1,0:T(8,128)(2,1)S(1)}, u32[]{:S(2)}, u32[]{:S(2)}) collective-permute-start(s16[336,128]{1,0:T(8,128)(2,1)} %get-tuple-element.26), channel_id=1, source_target_pairs={{0,8},{8,0},{1,9},{9,1},{2,10},{10,2},{3,11},{11,3},{4,12},{12,4},... | collective-permute-start | bytes 258056 | tf_op jit(solution)/shard_map/ppermute | solution.py:23
  41.3 2.9 %collective-permute-done.3.refs_1_ = s16[336,128]{1,0:T(8,128)(2,1)S(1)} collective-permute-done((s16[336,128]{1,0:T(8,128)(2,1)}, s16[336,128]{1,0:T(8,128)(2,1)S(1)}, u32[]{:S(2)}, u32[]{:S(2)}) %collective-permute-start.3) | collective-permute-done | bytes 86048 | tf_op jit(solution)/shard_map/ppermute | solution.py:23
  44.2 0.0 copy-start.3
  44.2 0.6 copy-done.3
  44.8 2.4 %level3.1 = (f32[320,128]{1,0:T(8,128)}, s16[336,128]{1,0:T(8,128)(2,1)}) custom-call(f32[320,128]{1,0:T(8,128)} %get-tuple-element.25.refs_0_, s16[336,128]{1,0:T(8,128)(2,1)} %copy-done.3, bf16[38,64,128]{2,1,0:T(8,128)(2,1)} %get-tuple-element.35.refs_2_), custom_call_target="tpu_custom_call" | custom-call | tf_op jit(solution)/shard_map/level3/pallas_call | solution.py:252
  47.3 17.9 %collective-permute-start.4 = (s16[336,128]{1,0:T(8,128)(2,1)}, s16[336,128]{1,0:T(8,128)(2,1)S(1)}, u32[]{:S(2)}, u32[]{:S(2)}) collective-permute-start(s16[336,128]{1,0:T(8,128)(2,1)} %get-tuple-element.28), channel_id=1, source_target_pairs={{0,16},{16,0},{1,17},{17,1},{2,18},{18,2},{3,19},{19,3},{4,20},{20... | collective-permute-start | bytes 258056 | tf_op jit(solution)/shard_map/ppermute | solution.py:23
  65.1 2.7 %collective-permute-done.4.refs_1_ = s16[336,128]{1,0:T(8,128)(2,1)S(1)} collective-permute-done((s16[336,128]{1,0:T(8,128)(2,1)}, s16[336,128]{1,0:T(8,128)(2,1)S(1)}, u32[]{:S(2)}, u32[]{:S(2)}) %collective-permute-start.4) | collective-permute-done | bytes 86048 | tf_op jit(solution)/shard_map/ppermute | solution.py:23
  67.8 0.0 copy-start.4
  67.8 0.6 copy-done.4
  68.4 2.5 %level4.1 = (f32[320,128]{1,0:T(8,128)}, s16[336,128]{1,0:T(8,128)(2,1)}) custom-call(f32[320,128]{1,0:T(8,128)} %get-tuple-element.27.refs_0_, s16[336,128]{1,0:T(8,128)(2,1)} %copy-done.4, bf16[38,64,128]{2,1,0:T(8,128)(2,1)} %get-tuple-element.34.refs_2_), custom_call_target="tpu_custom_call" | custom-call | tf_op jit(solution)/shard_map/level4/pallas_call | solution.py:252
  70.9 0.0 collective-permute-start.5
  70.9 5.6 %collective-permute-done.5.refs_1_ = s16[336,128]{1,0:T(8,128)(2,1)S(1)} collective-permute-done((s16[336,128]{1,0:T(8,128)(2,1)}, s16[336,128]{1,0:T(8,128)(2,1)S(1)}, u32[]{:S(2)}, u32[]{:S(2)}) %collective-permute-start.5) | collective-permute-done | bytes 86048 | tf_op jit(solution)/shard_map/ppermute | solution.py:23
  76.5 0.0 copy-start.5
  76.5 0.6 copy-done.5
  77.2 2.4 %level5.1 = (f32[320,128]{1,0:T(8,128)}, s16[336,128]{1,0:T(8,128)(2,1)}) custom-call(f32[320,128]{1,0:T(8,128)} %get-tuple-element.29.refs_0_, s16[336,128]{1,0:T(8,128)(2,1)} %copy-done.5, bf16[38,64,128]{2,1,0:T(8,128)(2,1)} %get-tuple-element.39.refs_2_), custom_call_target="tpu_custom_call" | custom-call | tf_op jit(solution)/shard_map/level5/pallas_call | solution.py:252
  79.6 0.0 collective-permute-start.6
  79.6 9.1 %collective-permute-done.6.refs_2_ = s16[336,128]{1,0:T(8,128)(2,1)S(1)} collective-permute-done((s16[336,128]{1,0:T(8,128)(2,1)}, s16[336,128]{1,0:T(8,128)(2,1)S(1)}, u32[]{:S(2)}, u32[]{:S(2)}) %collective-permute-start.6) | collective-permute-done | bytes 86048 | tf_op jit(solution)/shard_map/ppermute | solution.py:23
  88.7 0.0 copy-start.6
  88.7 0.6 copy-done.6
  89.3 2.9 %last.1 = f32[512,38]{1,0:T(8,128)} custom-call(s32[38]{0:T(128)} %refs_0_.3, f32[320,128]{1,0:T(8,128)} %get-tuple-element.31.refs_1_, s16[336,128]{1,0:T(8,128)(2,1)} %copy-done.6, bf16[38,64,128]{2,1,0:T(8,128)(2,1)} %get-tuple-element.33.refs_3_, bf16[38,32,64]{2,1,0:T(8,128)(2,1)} %bitcast.23), custom_call_target="tpu_custom_call" | custom-call | tf_op jit(solution)/shard_map/last/pallas_call | solution.py:261
Async XLA Ops:
  9.5 4.5 %collective-permute-start = (s16[336,128]{1,0:T(8,128)(2,1)}, s16[336,128]{1,0:T(8,128)(2,1)S(1)}, u32[]{:S(2)}, u32[]{:S(2)}) collective-permute-start(s16[336,128]{1,0:T(8,128)(2,1)} %get-tuple-element.20), channel_id=1, source_target_pairs={{0,1},{1,0},{2,3},{3,2},{4,5},{5,4},{6,7},{7,6},{8,9},{9,8},{10,11... | collective-permute-start | bytes 258056 | tf_op jit(solution)/shard_map/ppermute | solution.py:23
  14.0 0.6 copy-start
  17.0 5.1 %collective-permute-start.1 = (s16[336,128]{1,0:T(8,128)(2,1)}, s16[336,128]{1,0:T(8,128)(2,1)S(1)}, u32[]{:S(2)}, u32[]{:S(2)}) collective-permute-start(s16[336,128]{1,0:T(8,128)(2,1)} %get-tuple-element.22), channel_id=1, source_target_pairs={{0,2},{2,0},{1,3},{3,1},{4,6},{6,4},{5,7},{7,5},{8,10},{10,8},{9,1... | collective-permute-start | bytes 258056 | tf_op jit(solution)/shard_map/ppermute | solution.py:23
  22.2 0.6 copy-start.1
  25.2 7.2 %collective-permute-start.2 = (s16[336,128]{1,0:T(8,128)(2,1)}, s16[336,128]{1,0:T(8,128)(2,1)S(1)}, u32[]{:S(2)}, u32[]{:S(2)}) collective-permute-start(s16[336,128]{1,0:T(8,128)(2,1)} %get-tuple-element.24), channel_id=1, source_target_pairs={{0,4},{4,0},{1,5},{5,1},{2,6},{6,2},{3,7},{7,3},{8,12},{12,8},{9,1... | collective-permute-start | bytes 258056 | tf_op jit(solution)/shard_map/ppermute | solution.py:23
  32.4 0.6 copy-start.2
  35.5 8.8 %collective-permute-start.3 = (s16[336,128]{1,0:T(8,128)(2,1)}, s16[336,128]{1,0:T(8,128)(2,1)S(1)}, u32[]{:S(2)}, u32[]{:S(2)}) collective-permute-start(s16[336,128]{1,0:T(8,128)(2,1)} %get-tuple-element.26), channel_id=1, source_target_pairs={{0,8},{8,0},{1,9},{9,1},{2,10},{10,2},{3,11},{11,3},{4,12},{12,4},... | collective-permute-start | bytes 258056 | tf_op jit(solution)/shard_map/ppermute | solution.py:23
  44.2 0.6 copy-start.3
  47.3 20.6 %collective-permute-start.4 = (s16[336,128]{1,0:T(8,128)(2,1)}, s16[336,128]{1,0:T(8,128)(2,1)S(1)}, u32[]{:S(2)}, u32[]{:S(2)}) collective-permute-start(s16[336,128]{1,0:T(8,128)(2,1)} %get-tuple-element.28), channel_id=1, source_target_pairs={{0,16},{16,0},{1,17},{17,1},{2,18},{18,2},{3,19},{19,3},{4,20},{20... | collective-permute-start | bytes 258056 | tf_op jit(solution)/shard_map/ppermute | solution.py:23
  67.8 0.6 copy-start.4
  70.9 5.6 %collective-permute-start.5 = (s16[336,128]{1,0:T(8,128)(2,1)}, s16[336,128]{1,0:T(8,128)(2,1)S(1)}, u32[]{:S(2)}, u32[]{:S(2)}) collective-permute-start(s16[336,128]{1,0:T(8,128)(2,1)} %get-tuple-element.30), channel_id=1, source_target_pairs={{0,32},{32,0},{1,33},{33,1},{2,34},{34,2},{3,35},{35,3},{4,36},{36... | collective-permute-start | bytes 258056 | tf_op jit(solution)/shard_map/ppermute | solution.py:23
  76.5 0.6 copy-start.5
  79.6 9.1 %collective-permute-start.6 = (s16[336,128]{1,0:T(8,128)(2,1)}, s16[336,128]{1,0:T(8,128)(2,1)S(1)}, u32[]{:S(2)}, u32[]{:S(2)}) collective-permute-start(s16[336,128]{1,0:T(8,128)(2,1)} %get-tuple-element.32), channel_id=1, source_target_pairs={{0,64},{64,0},{1,65},{65,1},{2,66},{66,2},{3,67},{67,3},{4,68},{68... | collective-permute-start | bytes 258056 | tf_op jit(solution)/shard_map/ppermute | solution.py:23
  88.7 0.6 copy-start.6

commit v2 on v1

--- a/solution.py
+++ b/solution.py
@@ -71,7 +71,7 @@
     return chosen
 
 
-def analyse_kernel(ids_hbm, weights_hbm, leaf_hbm, grid_hbm, own_ref, send_ref,
+def analyse_kernel(ids_hbm, weights_hbm, leaf_hbm, transfer_hbm, last_hbm, grid_hbm, own_ref, send_ref, factors_ref, last_ref,
                    ids, weights, leaf, grid, table, turned, raw, sems, grid_sems, *, fields, pieces):
     rows, nlon = grid.shape
     orders, cycles, rank = leaf.shape
@@ -84,6 +84,8 @@
     ids_load = pltpu.make_async_copy(ids_hbm, ids, sems.at[0])
     weights_load = pltpu.make_async_copy(weights_hbm, weights, sems.at[1])
     leaf_load = pltpu.make_async_copy(leaf_hbm, leaf, sems.at[2])
+    factors_load = pltpu.make_async_copy(transfer_hbm, factors_ref, sems.at[3])
+    last_load = pltpu.make_async_copy(last_hbm, last_ref, sems.at[4])
     ids_load.start()
     loads[0].start()
     loads[1].start()
@@ -91,6 +93,8 @@
     leaf_load.start()
     for load in loads[2:]:
         load.start()
+    factors_load.start()
+    last_load.start()
     half = 48
     ids_load.wait()
     row = lax.broadcasted_iota(I32, (half, LANES), 0)
@@ -139,6 +143,8 @@
     for g in range(groups):
         own_ref[g * rank : (g + 1) * rank, :] = results[g]
     encode(results, send_ref)
+    factors_load.wait()
+    last_load.wait()
 
 
 def join(own_ref, got_ref, joined, upper, groups, rank):
@@ -170,7 +176,8 @@
     return results
 
 
-def level_kernel(own_ref, got_ref, factors, next_ref, send_ref, joined, *, level):
+def level_kernel(own_ref, got_ref, factors_ref, next_ref, send_ref, joined, *, level):
+    factors = factors_ref.at[level]
     orders, rank, _ = factors.shape
     groups = joined.shape[0]
     upper = (lax.axis_index("lat") >> level) & 1 == 1
@@ -181,7 +188,8 @@
     encode(results, send_ref)
 
 
-def last_kernel(ids, own_ref, got_ref, factors, degree_weight, out_ref, joined, *, level):
+def last_kernel(ids, own_ref, got_ref, factors_ref, degree_weight, out_ref, joined, *, level):
+    factors = factors_ref.at[level]
     orders, rank, _ = factors.shape
     groups = joined.shape[0]
     degrees = degree_weight.shape[1]
@@ -212,6 +220,14 @@
         out_ref[pl.ds(q, degrees, stride=slots), :] = value[:, :orders]
 
 
+def in_vmem(value):
+    return pltpu.with_memory_space_constraint(value, pltpu.VMEM)
+
+
+def in_hbm(value):
+    return pltpu.with_memory_space_constraint(value, pltpu.HBM)
+
+
 def body(grid, cycle_weights, order_ids, leaf_weight, transfer, degree_weight):
     cycles, fields, nlon = grid.shape
     orders, rank = leaf_weight.shape[1:]
@@ -221,17 +237,17 @@
     pieces = 8
     leaf = leaf_weight.transpose(1, 0, 2)
     last = degree_weight.transpose(1, 0, 2)
-    hbm = pl.BlockSpec(memory_space=pl.ANY)
+    hbm = pl.BlockSpec(memory_space=pltpu.HBM)
     vmem = pl.BlockSpec(memory_space=pltpu.VMEM)
     smem = pl.BlockSpec(memory_space=pltpu.SMEM)
-    own_type = jax.ShapeDtypeStruct((groups * rank, LANES), F32)
-    send_type = jax.ShapeDtypeStruct((groups * rank + 16, LANES), I16)
+    own_type = pltpu.VMEM((groups * rank, LANES), F32)
+    send_type = pltpu.VMEM((groups * rank + 16, LANES), I16)
     joined = pltpu.VMEM((groups, 4 * rank, LANES), BF16)
-    own, send = pl.pallas_call(
+    own, send, factors, last = pl.pallas_call(
         lambda *refs: analyse_kernel(*refs, fields=fields, pieces=pieces),
-        out_shape=(own_type, send_type),
-        in_specs=[hbm] * 4,
-        out_specs=(vmem, vmem),
+        out_shape=(own_type, send_type, pltpu.VMEM(transfer.shape[:1] + transfer.shape[2:], BF16), pltpu.VMEM(last.shape, BF16)),
+        in_specs=[hbm] * 6,
+        out_specs=(vmem,) * 4,
         scratch_shapes=[
             pltpu.SMEM((orders,), I32),
             pltpu.VMEM((1, cycles), F32),
@@ -240,14 +256,15 @@
             pltpu.VMEM((LANES, nlon), BF16),
             pltpu.VMEM((orders * rank, 2 * cycles), BF16),
             pltpu.VMEM((cycles * fields, LANES), F32),
-            pltpu.SemaphoreType.DMA((3,)),
+            pltpu.SemaphoreType.DMA((5,)),
             pltpu.SemaphoreType.DMA((pieces,)),
         ],
+        compiler_params=pltpu.CompilerParams(vmem_limit_bytes=32 * 2**20),
         name="analyse",
-    )(order_ids, cycle_weights.reshape(1, cycles), leaf, grid.reshape(cycles * fields, nlon))
+    )(*map(in_hbm, (order_ids, cycle_weights.reshape(1, cycles), leaf, transfer[:, 0], last, grid.reshape(cycles * fields, nlon))))
+    own, send, factors, last = map(in_vmem, (own, send, factors, last))
     for level in range(levels):
-        got = from_partner(send, "lat", level)
-        factors = transfer[level, 0]
+        got = in_vmem(from_partner(send, "lat", level))
         if level + 1 < levels:
             own, send = pl.pallas_call(
                 lambda *refs, level=level: level_kernel(*refs, level=level),
@@ -255,8 +272,10 @@
                 in_specs=[vmem, vmem, vmem],
                 out_specs=(vmem, vmem),
                 scratch_shapes=[joined],
+                compiler_params=pltpu.CompilerParams(vmem_limit_bytes=16 * 2**20),
                 name=f"level{level}",
             )(own, got, factors)
+            own, send = in_vmem(own), in_vmem(send)
         else:
             out = pl.pallas_call(
                 lambda *refs: last_kernel(*refs, level=level),
@@ -264,6 +283,7 @@
                 in_specs=[smem, vmem, vmem, vmem, vmem],
                 out_specs=vmem,
                 scratch_shapes=[joined],
+                compiler_params=pltpu.CompilerParams(vmem_limit_bytes=16 * 2**20),
                 name="last",
             )(order_ids, own, got, factors, last)
     return out.reshape(degrees, 2 * fields, orders).transpose(0, 2, 1)

time: 93.5 us -> 71.7 us (0.77); the launches traced: 92.2 us -> 71.6 us
  Pallas kernels: 26.9 us -> 13.8 us
  local copies, waits for them, and re-layouts: 8.73 us -> 0.01 us
  starting transfers between devices: 28.2 us -> 29.2 us
    pallas_call x6, Pallas kernels: 14.6 us -> 3.46 us  [body(): pl.pallas_call(lambda *refs, level=level: level_kernel(*refs, level=level...]
    unnamed x14 -> x2, local copies, waits for them, and re-layouts: 4.4 us -> 0.01 us
    squeeze x1 -> x0, local copies, waits for them, and re-layouts: 4.32 us -> none  [body(): factors = transfer[level, 0]]
    pallas_call x1, Pallas kernels: 9.48 us -> 8.25 us  [body(): pl.pallas_call(lambda *refs: analyse_kernel(*refs, fields=fields, pieces=...]
    ppermute x7, starting transfers between devices: 28.2 us -> 29.2 us  [from_partner(): return lax.ppermute(block, axis, route)]
  transfers between devices with their start and end apart: 7 -> 7, of which waited for: 6 -> 7; matrix products, arithmetic and copies ran while one was open for 5% -> 0% of each run, Pallas kernels for 0% -> 0%
where the time goes in v2:
time: 71.7 us; the launch traced here: 71.6 us
  starting transfers between devices  29.2 us (41%)
  waiting for transfers between devices  28.5 us (40%)
  Pallas kernels  13.8 us (19%)
    ppermute x7, starting transfers between devices, from_partner(): return lax.ppermute(block, axis, route)  29.2 us
    ppermute x7, waiting for transfers between devices, from_partner(): return lax.ppermute(block, axis, route)  28.5 us
    pallas_call x1, Pallas kernels, body(): pl.pallas_call(lambda *refs: analyse_kernel(*refs, fields=fields, pieces=...  8.25 us
    pallas_call x6, Pallas kernels, body(): pl.pallas_call(lambda *refs, level=level: level_kernel(*refs, level=level...  3.46 us
    pallas_call x1, Pallas kernels, body(): pl.pallas_call(lambda *refs: last_kernel(*refs, level=level), out_shape=j...  2.13 us
  transfers between devices with their start and end apart: 7, of which 7 were waited for; matrix products, arithmetic and copies ran while one was open for 0% of the time, Pallas kernels for 0%

profile of v2, /device:TPU:528, one launch (start us, length us, event | category | flops | bytes accessed | tf_op | source)
XLA Modules:
  0.0 71.6 jit_solution(6544509817843504009)
XLA Ops:
  0.0 8.2 %analyse.1 = (f32[320,128]{1,0:T(8,128)S(1)}, s16[336,128]{1,0:T(8,128)(2,1)S(1)}, bf16[7,38,64,128]{3,2,1,0:T(8,128)(2,1)S(1)}, bf16[38,32,64]{2,1,0:T(8,128)(2,1)S(1)}) custom-call(s32[38]{0:T(128)} %refs_0_.3, f32[1,64]{1,0:T(1,128)} %bitcast.12, bf16[38,64,64]{2,1,0:T(8,128)(2,1)} %bitcast.10, bf16[7,38,64,128]{3,2,1,0:T(8,128)(2,1)} %bitcast.9, ...), custom_call_target="tpu_custom_call" | custom-call | tf_op jit(solution)/shard_map/analyse/pallas_call | solution.py:246
  8.3 0.1 collective-permute-start
  8.4 1.3 %collective-permute-done.refs_1_ = s16[336,128]{1,0:T(8,128)(2,1)S(1)} collective-permute-done((s16[336,128]{1,0:T(8,128)(2,1)S(1)}, s16[336,128]{1,0:T(8,128)(2,1)S(1)}, u32[]{:S(2)}, u32[]{:S(2)}) %collective-permute-start) | collective-permute-done | bytes 86048 | tf_op jit(solution)/shard_map/ppermute | solution.py:23
  9.7 0.6 level0.1
  10.2 1.7 %collective-permute-start.1 = (s16[336,128]{1,0:T(8,128)(2,1)S(1)}, s16[336,128]{1,0:T(8,128)(2,1)S(1)}, u32[]{:S(2)}, u32[]{:S(2)}) collective-permute-start(s16[336,128]{1,0:T(8,128)(2,1)S(1)} %get-tuple-element.25), channel_id=1, source_target_pairs={{0,2},{2,0},{1,3},{3,1},{4,6},{6,4},{5,7},{7,5},{8,10},{10,8},{9,1... | collective-permute-start | bytes 258056 | tf_op jit(solution)/shard_map/ppermute | solution.py:23
  12.0 3.0 %collective-permute-done.1.refs_1_ = s16[336,128]{1,0:T(8,128)(2,1)S(1)} collective-permute-done((s16[336,128]{1,0:T(8,128)(2,1)S(1)}, s16[336,128]{1,0:T(8,128)(2,1)S(1)}, u32[]{:S(2)}, u32[]{:S(2)}) %collective-permute-start.1) | collective-permute-done | bytes 86048 | tf_op jit(solution)/shard_map/ppermute | solution.py:23
  15.0 0.6 level1.1
  15.5 2.8 %collective-permute-start.2 = (s16[336,128]{1,0:T(8,128)(2,1)S(1)}, s16[336,128]{1,0:T(8,128)(2,1)S(1)}, u32[]{:S(2)}, u32[]{:S(2)}) collective-permute-start(s16[336,128]{1,0:T(8,128)(2,1)S(1)} %get-tuple-element.27), channel_id=1, source_target_pairs={{0,4},{4,0},{1,5},{5,1},{2,6},{6,2},{3,7},{7,3},{8,12},{12,8},{9,1... | collective-permute-start | bytes 258056 | tf_op jit(solution)/shard_map/ppermute | solution.py:23
  18.4 4.0 %collective-permute-done.2.refs_1_ = s16[336,128]{1,0:T(8,128)(2,1)S(1)} collective-permute-done((s16[336,128]{1,0:T(8,128)(2,1)S(1)}, s16[336,128]{1,0:T(8,128)(2,1)S(1)}, u32[]{:S(2)}, u32[]{:S(2)}) %collective-permute-start.2) | collective-permute-done | bytes 86048 | tf_op jit(solution)/shard_map/ppermute | solution.py:23
  22.3 0.6 level2.1
  22.9 5.9 %collective-permute-start.3 = (s16[336,128]{1,0:T(8,128)(2,1)S(1)}, s16[336,128]{1,0:T(8,128)(2,1)S(1)}, u32[]{:S(2)}, u32[]{:S(2)}) collective-permute-start(s16[336,128]{1,0:T(8,128)(2,1)S(1)} %get-tuple-element.29), channel_id=1, source_target_pairs={{0,8},{8,0},{1,9},{9,1},{2,10},{10,2},{3,11},{11,3},{4,12},{12,4},... | collective-permute-start | bytes 258056 | tf_op jit(solution)/shard_map/ppermute | solution.py:23
  28.9 3.5 %collective-permute-done.3.refs_1_ = s16[336,128]{1,0:T(8,128)(2,1)S(1)} collective-permute-done((s16[336,128]{1,0:T(8,128)(2,1)S(1)}, s16[336,128]{1,0:T(8,128)(2,1)S(1)}, u32[]{:S(2)}, u32[]{:S(2)}) %collective-permute-start.3) | collective-permute-done | bytes 86048 | tf_op jit(solution)/shard_map/ppermute | solution.py:23
  32.3 0.6 level3.1
  32.9 18.3 %collective-permute-start.4 = (s16[336,128]{1,0:T(8,128)(2,1)S(1)}, s16[336,128]{1,0:T(8,128)(2,1)S(1)}, u32[]{:S(2)}, u32[]{:S(2)}) collective-permute-start(s16[336,128]{1,0:T(8,128)(2,1)S(1)} %get-tuple-element.31), channel_id=1, source_target_pairs={{0,16},{16,0},{1,17},{17,1},{2,18},{18,2},{3,19},{19,3},{4,20},{20... | collective-permute-start | bytes 258056 | tf_op jit(solution)/shard_map/ppermute | solution.py:23
  51.2 2.5 %collective-permute-done.4.refs_1_ = s16[336,128]{1,0:T(8,128)(2,1)S(1)} collective-permute-done((s16[336,128]{1,0:T(8,128)(2,1)S(1)}, s16[336,128]{1,0:T(8,128)(2,1)S(1)}, u32[]{:S(2)}, u32[]{:S(2)}) %collective-permute-start.4) | collective-permute-done | bytes 86048 | tf_op jit(solution)/shard_map/ppermute | solution.py:23
  53.7 0.0 copy-start
  53.7 0.6 level4.1
  54.3 0.1 collective-permute-start.5
  54.4 5.5 %collective-permute-done.5.refs_1_ = s16[336,128]{1,0:T(8,128)(2,1)S(1)} collective-permute-done((s16[336,128]{1,0:T(8,128)(2,1)S(1)}, s16[336,128]{1,0:T(8,128)(2,1)S(1)}, u32[]{:S(2)}, u32[]{:S(2)}) %collective-permute-start.5) | collective-permute-done | bytes 86048 | tf_op jit(solution)/shard_map/ppermute | solution.py:23
  59.9 0.6 level5.1
  60.5 0.1 collective-permute-start.6
  60.6 8.8 %collective-permute-done.6.refs_2_ = s16[336,128]{1,0:T(8,128)(2,1)S(1)} collective-permute-done((s16[336,128]{1,0:T(8,128)(2,1)S(1)}, s16[336,128]{1,0:T(8,128)(2,1)S(1)}, u32[]{:S(2)}, u32[]{:S(2)}) %collective-permute-start.6) | collective-permute-done | bytes 86048 | tf_op jit(solution)/shard_map/ppermute | solution.py:23
  69.4 0.0 copy-done
  69.4 2.1 %last.1 = f32[512,38]{1,0:T(8,128)} custom-call(s32[38]{0:T(128)S(1)} %copy-done, f32[320,128]{1,0:T(8,128)S(1)} %get-tuple-element.34.refs_1_, s16[336,128]{1,0:T(8,128)(2,1)S(1)} %collective-permute-done.6.refs_2_, bf16[7,38,64,128]{3,2,1,0:T(8,128)(2,1)S(1)} %get-tuple-element.23.refs_2_.refs_3_, bf16[38,32,64]{2,1,0:T(8,128)(2,1)S(1)} %get-tuple-element.36.refs_4_), custom_call_target="tpu_custom_call" | custom-call | tf_op jit(solution)/shard_map/last/pallas_call | solution.py:280
Async XLA Ops:
  8.3 1.4 %collective-permute-start = (s16[336,128]{1,0:T(8,128)(2,1)S(1)}, s16[336,128]{1,0:T(8,128)(2,1)S(1)}, u32[]{:S(2)}, u32[]{:S(2)}) collective-permute-start(s16[336,128]{1,0:T(8,128)(2,1)S(1)} %get-tuple-element.22), channel_id=1, source_target_pairs={{0,1},{1,0},{2,3},{3,2},{4,5},{5,4},{6,7},{7,6},{8,9},{9,8},{10,11... | collective-permute-start | bytes 258056 | tf_op jit(solution)/shard_map/ppermute | solution.py:23
  10.2 4.7 %collective-permute-start.1 = (s16[336,128]{1,0:T(8,128)(2,1)S(1)}, s16[336,128]{1,0:T(8,128)(2,1)S(1)}, u32[]{:S(2)}, u32[]{:S(2)}) collective-permute-start(s16[336,128]{1,0:T(8,128)(2,1)S(1)} %get-tuple-element.25), channel_id=1, source_target_pairs={{0,2},{2,0},{1,3},{3,1},{4,6},{6,4},{5,7},{7,5},{8,10},{10,8},{9,1... | collective-permute-start | bytes 258056 | tf_op jit(solution)/shard_map/ppermute | solution.py:23
  15.5 6.8 %collective-permute-start.2 = (s16[336,128]{1,0:T(8,128)(2,1)S(1)}, s16[336,128]{1,0:T(8,128)(2,1)S(1)}, u32[]{:S(2)}, u32[]{:S(2)}) collective-permute-start(s16[336,128]{1,0:T(8,128)(2,1)S(1)} %get-tuple-element.27), channel_id=1, source_target_pairs={{0,4},{4,0},{1,5},{5,1},{2,6},{6,2},{3,7},{7,3},{8,12},{12,8},{9,1... | collective-permute-start | bytes 258056 | tf_op jit(solution)/shard_map/ppermute | solution.py:23
  22.9 9.4 %collective-permute-start.3 = (s16[336,128]{1,0:T(8,128)(2,1)S(1)}, s16[336,128]{1,0:T(8,128)(2,1)S(1)}, u32[]{:S(2)}, u32[]{:S(2)}) collective-permute-start(s16[336,128]{1,0:T(8,128)(2,1)S(1)} %get-tuple-element.29), channel_id=1, source_target_pairs={{0,8},{8,0},{1,9},{9,1},{2,10},{10,2},{3,11},{11,3},{4,12},{12,4},... | collective-permute-start | bytes 258056 | tf_op jit(solution)/shard_map/ppermute | solution.py:23
  32.9 20.8 %collective-permute-start.4 = (s16[336,128]{1,0:T(8,128)(2,1)S(1)}, s16[336,128]{1,0:T(8,128)(2,1)S(1)}, u32[]{:S(2)}, u32[]{:S(2)}) collective-permute-start(s16[336,128]{1,0:T(8,128)(2,1)S(1)} %get-tuple-element.31), channel_id=1, source_target_pairs={{0,16},{16,0},{1,17},{17,1},{2,18},{18,2},{3,19},{19,3},{4,20},{20... | collective-permute-start | bytes 258056 | tf_op jit(solution)/shard_map/ppermute | solution.py:23
  53.7 15.8 %copy-start = (s32[38]{0:T(128)S(1)}, s32[38]{0:T(128)}, u32[]{:S(2)}) copy-start(s32[38]{0:T(128)} %refs_0_.3) | copy-start | bytes 460
  54.3 5.6 %collective-permute-start.5 = (s16[336,128]{1,0:T(8,128)(2,1)S(1)}, s16[336,128]{1,0:T(8,128)(2,1)S(1)}, u32[]{:S(2)}, u32[]{:S(2)}) collective-permute-start(s16[336,128]{1,0:T(8,128)(2,1)S(1)} %get-tuple-element.33), channel_id=1, source_target_pairs={{0,32},{32,0},{1,33},{33,1},{2,34},{34,2},{3,35},{35,3},{4,36},{36... | collective-permute-start | bytes 258056 | tf_op jit(solution)/shard_map/ppermute | solution.py:23
  60.5 9.0 %collective-permute-start.6 = (s16[336,128]{1,0:T(8,128)(2,1)S(1)}, s16[336,128]{1,0:T(8,128)(2,1)S(1)}, u32[]{:S(2)}, u32[]{:S(2)}) collective-permute-start(s16[336,128]{1,0:T(8,128)(2,1)S(1)} %get-tuple-element.35), channel_id=1, source_target_pairs={{0,64},{64,0},{1,65},{65,1},{2,66},{66,2},{3,67},{67,3},{4,68},{68... | collective-permute-start | bytes 258056 | tf_op jit(solution)/shard_map/ppermute | solution.py:23

commit v3 on v2

--- a/solution.py
+++ b/solution.py
@@ -59,8 +59,7 @@
     scale = jnp.concatenate([scale] * (rank // 8), 0)
     for g, value in enumerate(values):
         send[g * rank : (g + 1) * rank, :] = (value * scale).astype(I32).astype(I16)
-    both = jnp.concatenate([exponent, exponent], 0)
-    send[len(values) * rank :, :] = both.astype(I32).astype(I16)
+    send[len(values) * rank :, :] = exponent.astype(I32).astype(I16)
 
 
 def pick(product, rows):
@@ -71,30 +70,28 @@
     return chosen
 
 
-def analyse_kernel(ids_hbm, weights_hbm, leaf_hbm, transfer_hbm, last_hbm, grid_hbm, own_ref, send_ref, factors_ref, last_ref,
-                   ids, weights, leaf, grid, table, turned, raw, sems, grid_sems, *, fields, pieces):
+def analyse_kernel(ids_hbm, weights_hbm, leaf_hbm, transfer_hbm, grid_hbm, own_ref, send_ref, first_ref,
+                   ids, weights, leaf, grid, table, turned, raw, wave_c, wave_s, sems, grid_sems, *, fields, pieces, turn):
     rows, nlon = grid.shape
     orders, cycles, rank = leaf.shape
     piece = nlon // pieces
     groups = pl.cdiv(orders, BLOCK)
-    loads = []
-    for i in range(pieces):
-        cut = (slice(None), slice(i * piece, (i + 1) * piece))
-        loads.append(pltpu.make_async_copy(grid_hbm.at[cut], grid.at[cut], grid_sems.at[i]))
+
+    def load_of(i):
+        cut = (slice(None), pl.ds(pl.multiple_of(i * piece, piece), piece))
+        return pltpu.make_async_copy(grid_hbm.at[cut], grid.at[cut], grid_sems.at[i])
+
+    loads = [load_of(i) for i in range(pieces)]
     ids_load = pltpu.make_async_copy(ids_hbm, ids, sems.at[0])
     weights_load = pltpu.make_async_copy(weights_hbm, weights, sems.at[1])
     leaf_load = pltpu.make_async_copy(leaf_hbm, leaf, sems.at[2])
-    factors_load = pltpu.make_async_copy(transfer_hbm, factors_ref, sems.at[3])
-    last_load = pltpu.make_async_copy(last_hbm, last_ref, sems.at[4])
+    first_load = pltpu.make_async_copy(transfer_hbm.at[0], first_ref, sems.at[3])
     ids_load.start()
-    loads[0].start()
-    loads[1].start()
     weights_load.start()
     leaf_load.start()
-    for load in loads[2:]:
+    for load in loads:
         load.start()
-    factors_load.start()
-    last_load.start()
+    first_load.start()
     half = 48
     ids_load.wait()
     row = lax.broadcasted_iota(I32, (half, LANES), 0)
@@ -103,27 +100,41 @@
         order = jnp.where(row == o, ids[o], order)
     fine_c, fine_s = cos_sin(order * lanes_of((half, LANES)) & nlon - 1, nlon)
     coarse_c, coarse_s = cos_sin(order * (lanes_of((half, LANES)) * LANES) & nlon - 1, nlon)
-    turn_c = coarse_c[:, piece // LANES : piece // LANES + 1] + jnp.zeros((half, LANES), F32)
-    turn_s = coarse_s[:, piece // LANES : piece // LANES + 1] + jnp.zeros((half, LANES), F32)
-    for a in range(piece // LANES):
+    turn_c = coarse_c[:, turn // LANES : turn // LANES + 1] + jnp.zeros((half, LANES), F32)
+    turn_s = coarse_s[:, turn // LANES : turn // LANES + 1] + jnp.zeros((half, LANES), F32)
+    for a in range(turn // LANES):
         ca, sa = coarse_c[:, a : a + 1], coarse_s[:, a : a + 1]
-        c, s = ca * fine_c - sa * fine_s, sa * fine_c + ca * fine_s
-        for i in range(pieces):
-            at = slice(i * piece + a * LANES, i * piece + (a + 1) * LANES)
-            table[0:half, at] = c.astype(BF16)
-            table[64 : 64 + half, at] = (-s).astype(BF16)
-            if i + 1 < pieces:
-                c, s = c * turn_c - s * turn_s, s * turn_c + c * turn_s
+        at = slice(a * LANES, (a + 1) * LANES)
+        wave_c[:, at], wave_s[:, at] = ca * fine_c - sa * fine_s, sa * fine_c + ca * fine_s
+
+    def fill(i, carry):
+        for a in range(turn // LANES):
+            at = slice(a * LANES, (a + 1) * LANES)
+            to = pl.ds(pl.multiple_of(i * turn + a * LANES, LANES), LANES)
+            c, s = wave_c[:, at], wave_s[:, at]
+            table[0:half, to] = c.astype(BF16)
+            table[64 : 64 + half, to] = (-s).astype(BF16)
+            wave_c[:, at], wave_s[:, at] = c * turn_c - s * turn_s, s * turn_c + c * turn_s
+        return carry
+
+    lax.fori_loop(0, nlon // turn, fill, 0)
     weights_load.wait()
     leaf_load.wait()
-    for o in range(orders):
-        turned[o * rank : (o + 1) * rank, :] = jnp.concatenate([leaf[o], leaf[o]], 0).T
+    raw[:, :] = jnp.zeros(raw.shape, F32)
+    share = pl.cdiv(orders, pieces)
+
+    def multiply(i, carry):
+        load_of(i).wait()
+        at = pl.ds(pl.multiple_of(i * piece, piece), piece)
+        raw[:, :] += lax.dot_general(grid[:, at], table[:, at], (((1,), (1,)), ((), ())), preferred_element_type=F32)
+        begin = jnp.minimum(i * share, orders - share)
+        for u in range(share):
+            o = begin + u
+            turned[pl.ds(pl.multiple_of(o * rank, rank), rank), :] = jnp.concatenate([leaf[o], leaf[o]], 0).T
+        return carry
+
+    lax.fori_loop(0, pieces, multiply, 0)
     weight = jnp.broadcast_to(weights[:, :], (LANES, cycles)).T * F32(1.0 / math.sqrt(nlon))
-    for i in range(pieces):
-        loads[i].wait()
-        at = slice(i * piece, (i + 1) * piece)
-        part = lax.dot_general(grid[:, at], table[:, at], (((1,), (1,)), ((), ())), preferred_element_type=F32)
-        raw[:, :] = part if i == 0 else raw[:, :] + part
     moved = []
     for f in range(fields):
         value = raw[pl.ds(f, cycles, stride=fields), :] * weight
@@ -143,12 +154,11 @@
     for g in range(groups):
         own_ref[g * rank : (g + 1) * rank, :] = results[g]
     encode(results, send_ref)
-    factors_load.wait()
-    last_load.wait()
+    first_load.wait()
 
 
 def join(own_ref, got_ref, joined, upper, groups, rank):
-    exponent = got_ref[groups * rank :, :].astype(I32).astype(F32)[0:8]
+    exponent = got_ref[groups * rank :, :].astype(I32).astype(F32)
     scale = jnp.exp2(exponent) * F32(1.0 / CODE)
     scale = jnp.concatenate([scale] * (rank // 8), 0)
     for g in range(groups):
@@ -177,7 +187,7 @@
 
 
 def level_kernel(own_ref, got_ref, factors_ref, next_ref, send_ref, joined, *, level):
-    factors = factors_ref.at[level]
+    factors = factors_ref.at[level - 1] if level else factors_ref
     orders, rank, _ = factors.shape
     groups = joined.shape[0]
     upper = (lax.axis_index("lat") >> level) & 1 == 1
@@ -188,8 +198,27 @@
     encode(results, send_ref)
 
 
-def last_kernel(ids, own_ref, got_ref, factors_ref, degree_weight, out_ref, joined, *, level):
-    factors = factors_ref.at[level]
+def fetch_kernel(after_ref, ids_hbm, transfer_hbm, last_hbm, factors_ref, last_ref, lanes_ref, ids, sems):
+    del after_ref
+    ids_load = pltpu.make_async_copy(ids_hbm, ids, sems.at[0])
+    factors_load = pltpu.make_async_copy(transfer_hbm.at[1:], factors_ref, sems.at[1])
+    last_load = pltpu.make_async_copy(last_hbm, last_ref, sems.at[2])
+    ids_load.start()
+    factors_load.start()
+    last_load.start()
+    ids_load.wait()
+    lane = lanes_of((8, LANES)) % BLOCK
+    for g in range(lanes_ref.shape[0]):
+        order = jnp.zeros((8, LANES), I32)
+        for o in range(min(BLOCK, ids.shape[0] - g * BLOCK)):
+            order = jnp.where(lane == o, ids[g * BLOCK + o], order)
+        lanes_ref[g] = order
+    factors_load.wait()
+    last_load.wait()
+
+
+def last_kernel(lanes_ref, own_ref, got_ref, factors_ref, degree_weight, out_ref, joined, *, level):
+    factors = factors_ref.at[level - 1]
     orders, rank, _ = factors.shape
     groups = joined.shape[0]
     degrees = degree_weight.shape[1]
@@ -207,9 +236,7 @@
         high, low = split(finals[g])
         product = jnp.dot(left, jnp.concatenate([high, low], 1), preferred_element_type=F32)
         value = pick(product[:, :LANES] + product[:, LANES:], degrees)
-        order = jnp.zeros((degrees, LANES), I32)
-        for o in range(count):
-            order = jnp.where(lane % BLOCK == o, ids[g * BLOCK + o], order)
+        order = jnp.concatenate([lanes_ref[g]] * (degrees // 8), 0)
         outs.append(jnp.where(degree >= order, value, F32(0.0)))
     slot = lane // BLOCK
     for q in range(slots):
@@ -234,20 +261,19 @@
     levels = transfer.shape[0]
     degrees = degree_weight.shape[0]
     groups = -(-orders // BLOCK)
-    pieces = 8
+    pieces = 2
     leaf = leaf_weight.transpose(1, 0, 2)
     last = degree_weight.transpose(1, 0, 2)
     hbm = pl.BlockSpec(memory_space=pltpu.HBM)
     vmem = pl.BlockSpec(memory_space=pltpu.VMEM)
-    smem = pl.BlockSpec(memory_space=pltpu.SMEM)
     own_type = pltpu.VMEM((groups * rank, LANES), F32)
-    send_type = pltpu.VMEM((groups * rank + 16, LANES), I16)
+    send_type = pltpu.VMEM((groups * rank + 8, LANES), I16)
     joined = pltpu.VMEM((groups, 4 * rank, LANES), BF16)
-    own, send, factors, last = pl.pallas_call(
-        lambda *refs: analyse_kernel(*refs, fields=fields, pieces=pieces),
-        out_shape=(own_type, send_type, pltpu.VMEM(transfer.shape[:1] + transfer.shape[2:], BF16), pltpu.VMEM(last.shape, BF16)),
-        in_specs=[hbm] * 6,
-        out_specs=(vmem,) * 4,
+    own, send, first = pl.pallas_call(
+        lambda *refs: analyse_kernel(*refs, fields=fields, pieces=pieces, turn=1024),
+        out_shape=(own_type, send_type, pltpu.VMEM(transfer.shape[2:], BF16)),
+        in_specs=[hbm] * 5,
+        out_specs=(vmem,) * 3,
         scratch_shapes=[
             pltpu.SMEM((orders,), I32),
             pltpu.VMEM((1, cycles), F32),
@@ -256,13 +282,15 @@
             pltpu.VMEM((LANES, nlon), BF16),
             pltpu.VMEM((orders * rank, 2 * cycles), BF16),
             pltpu.VMEM((cycles * fields, LANES), F32),
-            pltpu.SemaphoreType.DMA((5,)),
+            pltpu.VMEM((48, 1024), F32),
+            pltpu.VMEM((48, 1024), F32),
+            pltpu.SemaphoreType.DMA((4,)),
             pltpu.SemaphoreType.DMA((pieces,)),
         ],
         compiler_params=pltpu.CompilerParams(vmem_limit_bytes=32 * 2**20),
         name="analyse",
-    )(*map(in_hbm, (order_ids, cycle_weights.reshape(1, cycles), leaf, transfer[:, 0], last, grid.reshape(cycles * fields, nlon))))
-    own, send, factors, last = map(in_vmem, (own, send, factors, last))
+    )(*map(in_hbm, (order_ids, cycle_weights.reshape(1, cycles), leaf, transfer[:, 0], grid.reshape(cycles * fields, nlon))))
+    own, send, first = map(in_vmem, (own, send, first))
     for level in range(levels):
         got = in_vmem(from_partner(send, "lat", level))
         if level + 1 < levels:
@@ -274,18 +302,32 @@
                 scratch_shapes=[joined],
                 compiler_params=pltpu.CompilerParams(vmem_limit_bytes=16 * 2**20),
                 name=f"level{level}",
-            )(own, got, factors)
+            )(own, got, factors if level else first)
             own, send = in_vmem(own), in_vmem(send)
+            if not level:
+                factors, last, order_lanes = map(in_vmem, pl.pallas_call(
+                    fetch_kernel,
+                    out_shape=(
+                        pltpu.VMEM((levels - 1,) + transfer.shape[2:], BF16),
+                        pltpu.VMEM(last.shape, BF16),
+                        pltpu.VMEM((groups, 8, LANES), I32),
+                    ),
+                    in_specs=[vmem] + [hbm] * 3,
+                    out_specs=(vmem,) * 3,
+                    scratch_shapes=[pltpu.SMEM((orders,), I32), pltpu.SemaphoreType.DMA((3,))],
+                    compiler_params=pltpu.CompilerParams(vmem_limit_bytes=16 * 2**20),
+                    name="fetch",
+                )(own, *map(in_hbm, (order_ids, transfer[:, 0], last))))
         else:
             out = pl.pallas_call(
                 lambda *refs: last_kernel(*refs, level=level),
                 out_shape=jax.ShapeDtypeStruct((degrees * 2 * fields, orders), F32),
-                in_specs=[smem, vmem, vmem, vmem, vmem],
+                in_specs=[vmem] * 5,
                 out_specs=vmem,
                 scratch_shapes=[joined],
                 compiler_params=pltpu.CompilerParams(vmem_limit_bytes=16 * 2**20),
                 name="last",
-            )(order_ids, own, got, factors, last)
+            )(order_lanes, own, got, factors, last)
     return out.reshape(degrees, 2 * fields, orders).transpose(0, 2, 1)
 
 

time: 71.7 us -> 68.1 us (0.950)
  waiting for transfers between devices: 28.5 us -> 26.1 us
  Pallas kernels: 13.8 us -> 12.7 us
    pallas_call x1, Pallas kernels: 8.25 us -> 5.54 us  [body(): pl.pallas_call(lambda *refs: analyse_kernel(*refs, fields=fields, pieces=...]
    ppermute x7, waiting for transfers between devices: 28.5 us -> 26.1 us  [from_partner(): return lax.ppermute(block, axis, route)]
    pallas_call x0 -> x1, Pallas kernels: none -> 2.12 us  [body(): pl.pallas_call(fetch_kernel, out_shape=(pltpu.VMEM((levels - 1,) + transf...]
  transfers between devices with their start and end apart: 7 -> 7, of which waited for: 7 -> 7; matrix products, arithmetic and copies ran while one was open for 0% -> 0% of each run, Pallas kernels for 0% -> 3%
where the time goes in v3:
time: 68.1 us; the launch traced here: 68 us
  starting transfers between devices  29.1 us (43%)
  waiting for transfers between devices  26.1 us (38%)
  Pallas kernels  12.7 us (19%)
    ppermute x7, starting transfers between devices, from_partner(): return lax.ppermute(block, axis, route)  29.1 us
    ppermute x7, waiting for transfers between devices, from_partner(): return lax.ppermute(block, axis, route)  26.1 us
    pallas_call x1, Pallas kernels, body(): pl.pallas_call(lambda *refs: analyse_kernel(*refs, fields=fields, pieces=...  5.54 us
    pallas_call x6, Pallas kernels, body(): pl.pallas_call(lambda *refs, level=level: level_kernel(*refs, level=level...  3.47 us
    pallas_call x1, Pallas kernels, body(): pl.pallas_call(fetch_kernel, out_shape=(pltpu.VMEM((levels - 1,) + transf...  2.12 us
    pallas_call x1, Pallas kernels, body(): pl.pallas_call(lambda *refs: last_kernel(*refs, level=level), out_shape=j...  1.59 us
  transfers between devices with their start and end apart: 7, of which 7 were waited for; matrix products, arithmetic and copies ran while one was open for 0% of the time, Pallas kernels for 3%

profile of v3, /device:TPU:528, one launch (start us, length us, event | category | flops | bytes accessed | tf_op | source)
XLA Modules:
  0.0 68.0 jit_solution(15696696670531830704)
XLA Ops:
  0.0 5.5 %analyse.1 = (f32[320,128]{1,0:T(8,128)S(1)}, s16[328,128]{1,0:T(8,128)(2,1)S(1)}, bf16[38,64,128]{2,1,0:T(8,128)(2,1)S(1)}) custom-call(s32[38]{0:T(128)} %ids_hbm.1, f32[1,64]{1,0:T(1,128)} %bitcast.13, bf16[38,64,64]{2,1,0:T(8,128)(2,1)} %bitcast.11, bf16[7,38,64,128]{3,2,1,0:T(8,128)(2,1)} %bitcast.8, bf16[512,8192]{1,0:T(8,128)(2,1)} %bitcast.10), custom_call_target="tpu_custom_call" | custom-call | tf_op jit(solution)/shard_map/analyse/pallas_call | solution.py:272
  5.6 0.1 collective-permute-start
  5.7 1.3 %collective-permute-done.refs_1_ = s16[328,128]{1,0:T(8,128)(2,1)S(1)} collective-permute-done((s16[328,128]{1,0:T(8,128)(2,1)S(1)}, s16[328,128]{1,0:T(8,128)(2,1)S(1)}, u32[]{:S(2)}, u32[]{:S(2)}) %collective-permute-start) | collective-permute-done | bytes 84000 | tf_op jit(solution)/shard_map/ppermute | solution.py:23
  7.0 0.6 level0.1
  7.5 1.8 %collective-permute-start.1 = (s16[328,128]{1,0:T(8,128)(2,1)S(1)}, s16[328,128]{1,0:T(8,128)(2,1)S(1)}, u32[]{:S(2)}, u32[]{:S(2)}) collective-permute-start(s16[328,128]{1,0:T(8,128)(2,1)S(1)} %get-tuple-element.28), channel_id=1, source_target_pairs={{0,2},{2,0},{1,3},{3,1},{4,6},{6,4},{5,7},{7,5},{8,10},{10,8},{9,1... | collective-permute-start | bytes 251912 | tf_op jit(solution)/shard_map/ppermute | solution.py:23
  9.3 2.1 %fetch.1 = (bf16[6,38,64,128]{3,2,1,0:T(8,128)(2,1)S(1)}, bf16[38,32,64]{2,1,0:T(8,128)(2,1)S(1)}, s32[5,8,128]{2,1,0:T(8,128)S(1)}) custom-call(f32[320,128]{1,0:T(8,128)S(1)} %get-tuple-element.26.after_ref.refs_0_, s32[38]{0:T(128)} %ids_hbm.1, bf16[7,38,64,128]{3,2,1,0:T(8,128)(2,1)} %bitcast.9, bf16[38,32,64]{2,1,0:T(8,128)(2,1)} %bitcast.12), custom_call_target="tpu_custom_call" | custom-call | tf_op jit(solution)/shard_map/fetch/pallas_call | solution.py:308
  11.4 0.8 %collective-permute-done.1.refs_1_ = s16[328,128]{1,0:T(8,128)(2,1)S(1)} collective-permute-done((s16[328,128]{1,0:T(8,128)(2,1)S(1)}, s16[328,128]{1,0:T(8,128)(2,1)S(1)}, u32[]{:S(2)}, u32[]{:S(2)}) %collective-permute-start.1) | collective-permute-done | bytes 84000 | tf_op jit(solution)/shard_map/ppermute | solution.py:23
  12.2 0.6 level1.1
  12.8 2.8 %collective-permute-start.2 = (s16[328,128]{1,0:T(8,128)(2,1)S(1)}, s16[328,128]{1,0:T(8,128)(2,1)S(1)}, u32[]{:S(2)}, u32[]{:S(2)}) collective-permute-start(s16[328,128]{1,0:T(8,128)(2,1)S(1)} %get-tuple-element.31), channel_id=1, source_target_pairs={{0,4},{4,0},{1,5},{5,1},{2,6},{6,2},{3,7},{7,3},{8,12},{12,8},{9,1... | collective-permute-start | bytes 251912 | tf_op jit(solution)/shard_map/ppermute | solution.py:23
  15.6 3.9 %collective-permute-done.2.refs_1_ = s16[328,128]{1,0:T(8,128)(2,1)S(1)} collective-permute-done((s16[328,128]{1,0:T(8,128)(2,1)S(1)}, s16[328,128]{1,0:T(8,128)(2,1)S(1)}, u32[]{:S(2)}, u32[]{:S(2)}) %collective-permute-start.2) | collective-permute-done | bytes 84000 | tf_op jit(solution)/shard_map/ppermute | solution.py:23
  19.5 0.6 level2.1
  20.1 5.9 %collective-permute-start.3 = (s16[328,128]{1,0:T(8,128)(2,1)S(1)}, s16[328,128]{1,0:T(8,128)(2,1)S(1)}, u32[]{:S(2)}, u32[]{:S(2)}) collective-permute-start(s16[328,128]{1,0:T(8,128)(2,1)S(1)} %get-tuple-element.33), channel_id=1, source_target_pairs={{0,8},{8,0},{1,9},{9,1},{2,10},{10,2},{3,11},{11,3},{4,12},{12,4},... | collective-permute-start | bytes 251912 | tf_op jit(solution)/shard_map/ppermute | solution.py:23
  26.1 3.5 %collective-permute-done.3.refs_1_ = s16[328,128]{1,0:T(8,128)(2,1)S(1)} collective-permute-done((s16[328,128]{1,0:T(8,128)(2,1)S(1)}, s16[328,128]{1,0:T(8,128)(2,1)S(1)}, u32[]{:S(2)}, u32[]{:S(2)}) %collective-permute-start.3) | collective-permute-done | bytes 84000 | tf_op jit(solution)/shard_map/ppermute | solution.py:23
  29.5 0.6 level3.1
  30.1 18.2 %collective-permute-start.4 = (s16[328,128]{1,0:T(8,128)(2,1)S(1)}, s16[328,128]{1,0:T(8,128)(2,1)S(1)}, u32[]{:S(2)}, u32[]{:S(2)}) collective-permute-start(s16[328,128]{1,0:T(8,128)(2,1)S(1)} %get-tuple-element.35), channel_id=1, source_target_pairs={{0,16},{16,0},{1,17},{17,1},{2,18},{18,2},{3,19},{19,3},{4,20},{20... | collective-permute-start | bytes 251912 | tf_op jit(solution)/shard_map/ppermute | solution.py:23
  48.3 2.5 %collective-permute-done.4.refs_1_ = s16[328,128]{1,0:T(8,128)(2,1)S(1)} collective-permute-done((s16[328,128]{1,0:T(8,128)(2,1)S(1)}, s16[328,128]{1,0:T(8,128)(2,1)S(1)}, u32[]{:S(2)}, u32[]{:S(2)}) %collective-permute-start.4) | collective-permute-done | bytes 84000 | tf_op jit(solution)/shard_map/ppermute | solution.py:23
  50.8 0.6 level4.1
  51.4 0.1 collective-permute-start.5
  51.5 5.4 %collective-permute-done.5.refs_1_ = s16[328,128]{1,0:T(8,128)(2,1)S(1)} collective-permute-done((s16[328,128]{1,0:T(8,128)(2,1)S(1)}, s16[328,128]{1,0:T(8,128)(2,1)S(1)}, u32[]{:S(2)}, u32[]{:S(2)}) %collective-permute-start.5) | collective-permute-done | bytes 84000 | tf_op jit(solution)/shard_map/ppermute | solution.py:23
  56.9 0.6 level5.1
  57.5 0.1 collective-permute-start.6
  57.7 8.8 %collective-permute-done.6.refs_2_ = s16[328,128]{1,0:T(8,128)(2,1)S(1)} collective-permute-done((s16[328,128]{1,0:T(8,128)(2,1)S(1)}, s16[328,128]{1,0:T(8,128)(2,1)S(1)}, u32[]{:S(2)}, u32[]{:S(2)}) %collective-permute-start.6) | collective-permute-done | bytes 84000 | tf_op jit(solution)/shard_map/ppermute | solution.py:23
  66.4 1.6 %last.1 = f32[512,38]{1,0:T(8,128)} custom-call(s32[5,8,128]{2,1,0:T(8,128)S(1)} %get-tuple-element.27.refs_0_, f32[320,128]{1,0:T(8,128)S(1)} %get-tuple-element.38.refs_1_, s16[328,128]{1,0:T(8,128)(2,1)S(1)} %collective-permute-done.6.refs_2_, bf16[6,38,64,128]{3,2,1,0:T(8,128)(2,1)S(1)} %get-tuple-element.29.refs_2_.refs_3_, ...), custom_call_target="tpu_custom_call" | custom-call | tf_op jit(solution)/shard_map/last/pallas_call | solution.py:322
Async XLA Ops:
  5.6 1.4 %collective-permute-start = (s16[328,128]{1,0:T(8,128)(2,1)S(1)}, s16[328,128]{1,0:T(8,128)(2,1)S(1)}, u32[]{:S(2)}, u32[]{:S(2)}) collective-permute-start(s16[328,128]{1,0:T(8,128)(2,1)S(1)} %get-tuple-element.24), channel_id=1, source_target_pairs={{0,1},{1,0},{2,3},{3,2},{4,5},{5,4},{6,7},{7,6},{8,9},{9,8},{10,11... | collective-permute-start | bytes 251912 | tf_op jit(solution)/shard_map/ppermute | solution.py:23
  7.5 4.7 %collective-permute-start.1 = (s16[328,128]{1,0:T(8,128)(2,1)S(1)}, s16[328,128]{1,0:T(8,128)(2,1)S(1)}, u32[]{:S(2)}, u32[]{:S(2)}) collective-permute-start(s16[328,128]{1,0:T(8,128)(2,1)S(1)} %get-tuple-element.28), channel_id=1, source_target_pairs={{0,2},{2,0},{1,3},{3,1},{4,6},{6,4},{5,7},{7,5},{8,10},{10,8},{9,1... | collective-permute-start | bytes 251912 | tf_op jit(solution)/shard_map/ppermute | solution.py:23
  12.8 6.7 %collective-permute-start.2 = (s16[328,128]{1,0:T(8,128)(2,1)S(1)}, s16[328,128]{1,0:T(8,128)(2,1)S(1)}, u32[]{:S(2)}, u32[]{:S(2)}) collective-permute-start(s16[328,128]{1,0:T(8,128)(2,1)S(1)} %get-tuple-element.31), channel_id=1, source_target_pairs={{0,4},{4,0},{1,5},{5,1},{2,6},{6,2},{3,7},{7,3},{8,12},{12,8},{9,1... | collective-permute-start | bytes 251912 | tf_op jit(solution)/shard_map/ppermute | solution.py:23
  20.1 9.4 %collective-permute-start.3 = (s16[328,128]{1,0:T(8,128)(2,1)S(1)}, s16[328,128]{1,0:T(8,128)(2,1)S(1)}, u32[]{:S(2)}, u32[]{:S(2)}) collective-permute-start(s16[328,128]{1,0:T(8,128)(2,1)S(1)} %get-tuple-element.33), channel_id=1, source_target_pairs={{0,8},{8,0},{1,9},{9,1},{2,10},{10,2},{3,11},{11,3},{4,12},{12,4},... | collective-permute-start | bytes 251912 | tf_op jit(solution)/shard_map/ppermute | solution.py:23
  30.1 20.7 %collective-permute-start.4 = (s16[328,128]{1,0:T(8,128)(2,1)S(1)}, s16[328,128]{1,0:T(8,128)(2,1)S(1)}, u32[]{:S(2)}, u32[]{:S(2)}) collective-permute-start(s16[328,128]{1,0:T(8,128)(2,1)S(1)} %get-tuple-element.35), channel_id=1, source_target_pairs={{0,16},{16,0},{1,17},{17,1},{2,18},{18,2},{3,19},{19,3},{4,20},{20... | collective-permute-start | bytes 251912 | tf_op jit(solution)/shard_map/ppermute | solution.py:23
  51.4 5.5 %collective-permute-start.5 = (s16[328,128]{1,0:T(8,128)(2,1)S(1)}, s16[328,128]{1,0:T(8,128)(2,1)S(1)}, u32[]{:S(2)}, u32[]{:S(2)}) collective-permute-start(s16[328,128]{1,0:T(8,128)(2,1)S(1)} %get-tuple-element.37), channel_id=1, source_target_pairs={{0,32},{32,0},{1,33},{33,1},{2,34},{34,2},{3,35},{35,3},{4,36},{36... | collective-permute-start | bytes 251912 | tf_op jit(solution)/shard_map/ppermute | solution.py:23
  57.5 8.9 %collective-permute-start.6 = (s16[328,128]{1,0:T(8,128)(2,1)S(1)}, s16[328,128]{1,0:T(8,128)(2,1)S(1)}, u32[]{:S(2)}, u32[]{:S(2)}) collective-permute-start(s16[328,128]{1,0:T(8,128)(2,1)S(1)} %get-tuple-element.39), channel_id=1, source_target_pairs={{0,64},{64,0},{1,65},{65,1},{2,66},{66,2},{3,67},{67,3},{4,68},{68... | collective-permute-start | bytes 251912 | tf_op jit(solution)/shard_map/ppermute | solution.py:23

commit v4 on v3

--- a/solution.py
+++ b/solution.py
@@ -62,12 +62,19 @@
     send[len(values) * rank :, :] = exponent.astype(I32).astype(I16)
 
 
-def pick(product, rows):
-    lane = lanes_of((rows, LANES)) % BLOCK
+def pick(product, rows, share):
+    product = product[:, :LANES] + product[:, LANES:]
+    place = lanes_of((rows, LANES)) % BLOCK // share
     chosen = jnp.zeros((rows, LANES), F32)
     for o in range(product.shape[0] // rows):
-        chosen = jnp.where(lane == o, product[o * rows : (o + 1) * rows], chosen)
+        chosen = jnp.where(place == o, product[o * rows : (o + 1) * rows], chosen)
     return chosen
+
+
+def spread(value, share):
+    halves = jnp.concatenate(split(value), 1)
+    place = lanes_of(halves.shape) % share
+    return [halves * jnp.where(place == o, F32(1.0), F32(0.0)).astype(BF16) for o in range(share)]
 
 
 def analyse_kernel(ids_hbm, weights_hbm, leaf_hbm, transfer_hbm, grid_hbm, own_ref, send_ref, first_ref,
@@ -121,16 +128,17 @@
     weights_load.wait()
     leaf_load.wait()
     raw[:, :] = jnp.zeros(raw.shape, F32)
-    share = pl.cdiv(orders, pieces)
+    share = pl.cdiv(orders // 2, pieces)
+    turned[orders // 2 * rank :, :] = jnp.zeros((turned.shape[0] - orders // 2 * rank, 2 * cycles), BF16)
 
     def multiply(i, carry):
         load_of(i).wait()
         at = pl.ds(pl.multiple_of(i * piece, piece), piece)
         raw[:, :] += lax.dot_general(grid[:, at], table[:, at], (((1,), (1,)), ((), ())), preferred_element_type=F32)
-        begin = jnp.minimum(i * share, orders - share)
+        begin = jnp.minimum(i * share, orders // 2 - share)
         for u in range(share):
             o = begin + u
-            turned[pl.ds(pl.multiple_of(o * rank, rank), rank), :] = jnp.concatenate([leaf[o], leaf[o]], 0).T
+            turned[pl.ds(pl.multiple_of(o * rank, rank), rank), :] = jnp.concatenate([leaf[2 * o], leaf[2 * o + 1]], 0).T
         return carry
 
     lax.fori_loop(0, pieces, multiply, 0)
@@ -146,11 +154,10 @@
         waves = moved[0]
         for f in range(1, fields):
             waves = jnp.where(here == f, moved[f], waves)
-        high, low = split(waves)
-        count = min(BLOCK, orders - g * BLOCK)
-        at = slice(g * BLOCK * rank, (g * BLOCK + count) * rank)
-        product = jnp.dot(turned[at, :], jnp.concatenate([high, low], 0), preferred_element_type=F32)
-        results.append(pick(product, rank))
+        pairs = [turned[p * rank : (p + 1) * rank, :] for p in range(g * BLOCK // 2, (g + 1) * BLOCK // 2)]
+        left = jnp.concatenate([jnp.concatenate(pairs[p : p + 2], 1) for p in range(0, len(pairs), 2)], 0)
+        product = jnp.dot(left, jnp.concatenate(spread(waves, 4), 0), preferred_element_type=F32)
+        results.append(pick(product, rank, 4))
     for g in range(groups):
         own_ref[g * rank : (g + 1) * rank, :] = results[g]
     encode(results, send_ref)
@@ -165,24 +172,20 @@
         at = slice(g * rank, (g + 1) * rank)
         own = own_ref[at, :]
         other = got_ref[at, :].astype(I32).astype(F32) * scale
-        lower_half = jnp.where(upper, other, own)
-        upper_half = jnp.where(upper, own, other)
-        low_high, low_low = split(lower_half)
-        up_high, up_low = split(upper_half)
-        joined[g, 0:rank, :] = low_high
-        joined[g, rank : 2 * rank, :] = up_high
-        joined[g, 2 * rank : 3 * rank, :] = low_low
-        joined[g, 3 * rank : 4 * rank, :] = up_low
+        for o, value in enumerate(spread(jnp.where(upper, other, own), 2)):
+            joined[g, 2 * o * rank : (2 * o + 1) * rank, :] = value
+        for o, value in enumerate(spread(jnp.where(upper, own, other), 2)):
+            joined[g, (2 * o + 1) * rank : (2 * o + 2) * rank, :] = value
 
 
 def merge(factors, joined, groups):
     orders, rank, wide = factors.shape
     results = []
     for g in range(groups):
-        count = min(BLOCK, orders - g * BLOCK)
-        left = factors[g * BLOCK : g * BLOCK + count].reshape(count * rank, wide)
-        product = jnp.dot(jnp.concatenate([left, left], 1), joined[g], preferred_element_type=F32)
-        results.append(pick(product, rank))
+        first = range(g * BLOCK, min((g + 1) * BLOCK, orders), 2)
+        left = jnp.concatenate([jnp.concatenate([factors[o], factors[o + 1]], 1) for o in first], 0)
+        product = jnp.dot(left, joined[g], preferred_element_type=F32)
+        results.append(pick(product, rank, 2))
     return results
 
 
@@ -198,7 +201,7 @@
     encode(results, send_ref)
 
 
-def fetch_kernel(after_ref, ids_hbm, transfer_hbm, last_hbm, factors_ref, last_ref, lanes_ref, ids, sems):
+def fetch_kernel(after_ref, ids_hbm, transfer_hbm, last_hbm, factors_ref, quads_ref, lanes_ref, ids, last_ref, sems):
     del after_ref
     ids_load = pltpu.make_async_copy(ids_hbm, ids, sems.at[0])
     factors_load = pltpu.make_async_copy(transfer_hbm.at[1:], factors_ref, sems.at[1])
@@ -213,15 +216,20 @@
         for o in range(min(BLOCK, ids.shape[0] - g * BLOCK)):
             order = jnp.where(lane == o, ids[g * BLOCK + o], order)
         lanes_ref[g] = order
+    last_load.wait()
+    orders, degrees, rank = last_ref.shape
+    quads_ref[orders // 4 * degrees :, :] = jnp.zeros((quads_ref.shape[0] - orders // 4 * degrees, 4 * rank), BF16)
+    for o in range(0, orders, 2):
+        at = slice(o // 4 * degrees, (o // 4 + 1) * degrees)
+        quads_ref[at, o % 4 * rank : (o % 4 + 2) * rank] = jnp.concatenate([last_ref[o], last_ref[o + 1]], 1)
     factors_load.wait()
-    last_load.wait()
-
-
-def last_kernel(lanes_ref, own_ref, got_ref, factors_ref, degree_weight, out_ref, joined, *, level):
+
+
+def last_kernel(lanes_ref, own_ref, got_ref, factors_ref, quads_ref, out_ref, joined, *, level):
     factors = factors_ref.at[level - 1]
     orders, rank, _ = factors.shape
     groups = joined.shape[0]
-    degrees = degree_weight.shape[1]
+    degrees = quads_ref.shape[0] * 4 // (groups * BLOCK)
     slots = LANES // BLOCK
     position = lax.axis_index("lat")
     upper = (position >> level) & 1 == 1
@@ -231,11 +239,9 @@
     degree = position * degrees + lax.broadcasted_iota(I32, (degrees, LANES), 0)
     outs = []
     for g in range(groups):
-        count = min(BLOCK, orders - g * BLOCK)
-        left = degree_weight[g * BLOCK : g * BLOCK + count].reshape(count * degrees, rank)
-        high, low = split(finals[g])
-        product = jnp.dot(left, jnp.concatenate([high, low], 1), preferred_element_type=F32)
-        value = pick(product[:, :LANES] + product[:, LANES:], degrees)
+        left = quads_ref[2 * g * degrees : 2 * (g + 1) * degrees, :]
+        product = jnp.dot(left, jnp.concatenate(spread(finals[g], 4), 0), preferred_element_type=F32)
+        value = pick(product, degrees, 4)
         order = jnp.concatenate([lanes_ref[g]] * (degrees // 8), 0)
         outs.append(jnp.where(degree >= order, value, F32(0.0)))
     slot = lane // BLOCK
@@ -268,7 +274,7 @@
     vmem = pl.BlockSpec(memory_space=pltpu.VMEM)
     own_type = pltpu.VMEM((groups * rank, LANES), F32)
     send_type = pltpu.VMEM((groups * rank + 8, LANES), I16)
-    joined = pltpu.VMEM((groups, 4 * rank, LANES), BF16)
+    joined = pltpu.VMEM((groups, 4 * rank, 2 * LANES), BF16)
     own, send, first = pl.pallas_call(
         lambda *refs: analyse_kernel(*refs, fields=fields, pieces=pieces, turn=1024),
         out_shape=(own_type, send_type, pltpu.VMEM(transfer.shape[2:], BF16)),
@@ -280,7 +286,7 @@
             pltpu.VMEM((orders, cycles, rank), BF16),
             pltpu.VMEM((cycles * fields, nlon), BF16),
             pltpu.VMEM((LANES, nlon), BF16),
-            pltpu.VMEM((orders * rank, 2 * cycles), BF16),
+            pltpu.VMEM((groups * BLOCK // 2 * rank, 2 * cycles), BF16),
             pltpu.VMEM((cycles * fields, LANES), F32),
             pltpu.VMEM((48, 1024), F32),
             pltpu.VMEM((48, 1024), F32),
@@ -305,16 +311,16 @@
             )(own, got, factors if level else first)
             own, send = in_vmem(own), in_vmem(send)
             if not level:
-                factors, last, order_lanes = map(in_vmem, pl.pallas_call(
+                factors, quads, order_lanes = map(in_vmem, pl.pallas_call(
                     fetch_kernel,
                     out_shape=(
                         pltpu.VMEM((levels - 1,) + transfer.shape[2:], BF16),
-                        pltpu.VMEM(last.shape, BF16),
+                        pltpu.VMEM((groups * 2 * degrees, 4 * rank), BF16),
                         pltpu.VMEM((groups, 8, LANES), I32),
                     ),
                     in_specs=[vmem] + [hbm] * 3,
                     out_specs=(vmem,) * 3,
-                    scratch_shapes=[pltpu.SMEM((orders,), I32), pltpu.SemaphoreType.DMA((3,))],
+                    scratch_shapes=[pltpu.SMEM((orders,), I32), pltpu.VMEM(last.shape, BF16), pltpu.SemaphoreType.DMA((3,))],
                     compiler_params=pltpu.CompilerParams(vmem_limit_bytes=16 * 2**20),
                     name="fetch",
                 )(own, *map(in_hbm, (order_ids, transfer[:, 0], last))))
@@ -327,7 +333,7 @@
                 scratch_shapes=[joined],
                 compiler_params=pltpu.CompilerParams(vmem_limit_bytes=16 * 2**20),
                 name="last",
-            )(order_lanes, own, got, factors, last)
+            )(order_lanes, own, got, factors, quads)
     return out.reshape(degrees, 2 * fields, orders).transpose(0, 2, 1)
 
 

time: 68.1 us -> 66.8 us (0.981)
  Pallas kernels: 12.7 us -> 11.5 us
    pallas_call x6, Pallas kernels: 3.47 us -> 2.4 us  [body(): pl.pallas_call(lambda *refs, level=level: level_kernel(*refs, level=level...]
where the time goes in v4:
time: 66.8 us; the launch traced here: 66.7 us
  starting transfers between devices  29.1 us (44%)
  waiting for transfers between devices  25.9 us (39%)
  Pallas kernels  11.5 us (17%)
    ppermute x7, starting transfers between devices, from_partner(): return lax.ppermute(block, axis, route)  29.1 us
    ppermute x7, waiting for transfers between devices, from_partner(): return lax.ppermute(block, axis, route)  25.9 us
    pallas_call x1, Pallas kernels, body(): pl.pallas_call(lambda *refs: analyse_kernel(*refs, fields=fields, pieces=...  5.49 us
    pallas_call x6, Pallas kernels, body(): pl.pallas_call(lambda *refs, level=level: level_kernel(*refs, level=level...  2.4 us
    pallas_call x1, Pallas kernels, body(): pl.pallas_call(fetch_kernel, out_shape=(pltpu.VMEM((levels - 1,) + transf...  2.23 us
    pallas_call x1, Pallas kernels, body(): pl.pallas_call(lambda *refs: last_kernel(*refs, level=level), out_shape=j...  1.4 us
  transfers between devices with their start and end apart: 7, of which 7 were waited for; matrix products, arithmetic and copies ran while one was open for 0% of the time, Pallas kernels for 3%

profile of v4, /device:TPU:528, one launch (start us, length us, event | category | flops | bytes accessed | tf_op | source)
XLA Modules:
  0.0 66.7 jit_solution(17788209617675393456)
XLA Ops:
  0.0 5.5 %analyse.1 = (f32[320,128]{1,0:T(8,128)S(1)}, s16[328,128]{1,0:T(8,128)(2,1)S(1)}, bf16[38,64,128]{2,1,0:T(8,128)(2,1)S(1)}) custom-call(s32[38]{0:T(128)} %ids_hbm.1, f32[1,64]{1,0:T(1,128)} %bitcast.13, bf16[38,64,64]{2,1,0:T(8,128)(2,1)} %bitcast.11, bf16[7,38,64,128]{3,2,1,0:T(8,128)(2,1)} %bitcast.8, bf16[512,8192]{1,0:T(8,128)(2,1)} %bitcast.10), custom_call_target="tpu_custom_call" | custom-call | tf_op jit(solution)/shard_map/analyse/pallas_call | solution.py:278
  5.5 0.1 collective-permute-start
  5.6 1.3 %collective-permute-done.refs_1_ = s16[328,128]{1,0:T(8,128)(2,1)S(1)} collective-permute-done((s16[328,128]{1,0:T(8,128)(2,1)S(1)}, s16[328,128]{1,0:T(8,128)(2,1)S(1)}, u32[]{:S(2)}, u32[]{:S(2)}) %collective-permute-start) | collective-permute-done | bytes 84000 | tf_op jit(solution)/shard_map/ppermute | solution.py:23
  6.9 0.4 level0.1
  7.3 1.8 %collective-permute-start.1 = (s16[328,128]{1,0:T(8,128)(2,1)S(1)}, s16[328,128]{1,0:T(8,128)(2,1)S(1)}, u32[]{:S(2)}, u32[]{:S(2)}) collective-permute-start(s16[328,128]{1,0:T(8,128)(2,1)S(1)} %get-tuple-element.28), channel_id=1, source_target_pairs={{0,2},{2,0},{1,3},{3,1},{4,6},{6,4},{5,7},{7,5},{8,10},{10,8},{9,1... | collective-permute-start | bytes 251912 | tf_op jit(solution)/shard_map/ppermute | solution.py:23
  9.1 2.2 %fetch.1 = (bf16[6,38,64,128]{3,2,1,0:T(8,128)(2,1)S(1)}, bf16[320,256]{1,0:T(8,128)(2,1)S(1)}, s32[5,8,128]{2,1,0:T(8,128)S(1)}) custom-call(f32[320,128]{1,0:T(8,128)S(1)} %get-tuple-element.26.after_ref.refs_0_, s32[38]{0:T(128)} %ids_hbm.1, bf16[7,38,64,128]{3,2,1,0:T(8,128)(2,1)} %bitcast.9, bf16[38,32,64]{2,1,0:T(8,128)(2,1)} %bitcast.12), custom_call_target="tpu_custom_call" | custom-call | tf_op jit(solution)/shard_map/fetch/pallas_call | solution.py:314
  11.3 0.7 %collective-permute-done.1.refs_1_ = s16[328,128]{1,0:T(8,128)(2,1)S(1)} collective-permute-done((s16[328,128]{1,0:T(8,128)(2,1)S(1)}, s16[328,128]{1,0:T(8,128)(2,1)S(1)}, u32[]{:S(2)}, u32[]{:S(2)}) %collective-permute-start.1) | collective-permute-done | bytes 84000 | tf_op jit(solution)/shard_map/ppermute | solution.py:23
  12.0 0.4 level1.1
  12.4 2.8 %collective-permute-start.2 = (s16[328,128]{1,0:T(8,128)(2,1)S(1)}, s16[328,128]{1,0:T(8,128)(2,1)S(1)}, u32[]{:S(2)}, u32[]{:S(2)}) collective-permute-start(s16[328,128]{1,0:T(8,128)(2,1)S(1)} %get-tuple-element.31), channel_id=1, source_target_pairs={{0,4},{4,0},{1,5},{5,1},{2,6},{6,2},{3,7},{7,3},{8,12},{12,8},{9,1... | collective-permute-start | bytes 251912 | tf_op jit(solution)/shard_map/ppermute | solution.py:23
  15.2 3.9 %collective-permute-done.2.refs_1_ = s16[328,128]{1,0:T(8,128)(2,1)S(1)} collective-permute-done((s16[328,128]{1,0:T(8,128)(2,1)S(1)}, s16[328,128]{1,0:T(8,128)(2,1)S(1)}, u32[]{:S(2)}, u32[]{:S(2)}) %collective-permute-start.2) | collective-permute-done | bytes 84000 | tf_op jit(solution)/shard_map/ppermute | solution.py:23
  19.1 0.4 level2.1
  19.5 5.9 %collective-permute-start.3 = (s16[328,128]{1,0:T(8,128)(2,1)S(1)}, s16[328,128]{1,0:T(8,128)(2,1)S(1)}, u32[]{:S(2)}, u32[]{:S(2)}) collective-permute-start(s16[328,128]{1,0:T(8,128)(2,1)S(1)} %get-tuple-element.33), channel_id=1, source_target_pairs={{0,8},{8,0},{1,9},{9,1},{2,10},{10,2},{3,11},{11,3},{4,12},{12,4},... | collective-permute-start | bytes 251912 | tf_op jit(solution)/shard_map/ppermute | solution.py:23
  25.5 3.5 %collective-permute-done.3.refs_1_ = s16[328,128]{1,0:T(8,128)(2,1)S(1)} collective-permute-done((s16[328,128]{1,0:T(8,128)(2,1)S(1)}, s16[328,128]{1,0:T(8,128)(2,1)S(1)}, u32[]{:S(2)}, u32[]{:S(2)}) %collective-permute-start.3) | collective-permute-done | bytes 84000 | tf_op jit(solution)/shard_map/ppermute | solution.py:23
  28.9 0.4 level3.1
  29.3 18.2 %collective-permute-start.4 = (s16[328,128]{1,0:T(8,128)(2,1)S(1)}, s16[328,128]{1,0:T(8,128)(2,1)S(1)}, u32[]{:S(2)}, u32[]{:S(2)}) collective-permute-start(s16[328,128]{1,0:T(8,128)(2,1)S(1)} %get-tuple-element.35), channel_id=1, source_target_pairs={{0,16},{16,0},{1,17},{17,1},{2,18},{18,2},{3,19},{19,3},{4,20},{20... | collective-permute-start | bytes 251912 | tf_op jit(solution)/shard_map/ppermute | solution.py:23
  47.6 2.5 %collective-permute-done.4.refs_1_ = s16[328,128]{1,0:T(8,128)(2,1)S(1)} collective-permute-done((s16[328,128]{1,0:T(8,128)(2,1)S(1)}, s16[328,128]{1,0:T(8,128)(2,1)S(1)}, u32[]{:S(2)}, u32[]{:S(2)}) %collective-permute-start.4) | collective-permute-done | bytes 84000 | tf_op jit(solution)/shard_map/ppermute | solution.py:23
  50.0 0.4 level4.1
  50.4 0.1 collective-permute-start.5
  50.6 5.4 %collective-permute-done.5.refs_1_ = s16[328,128]{1,0:T(8,128)(2,1)S(1)} collective-permute-done((s16[328,128]{1,0:T(8,128)(2,1)S(1)}, s16[328,128]{1,0:T(8,128)(2,1)S(1)}, u32[]{:S(2)}, u32[]{:S(2)}) %collective-permute-start.5) | collective-permute-done | bytes 84000 | tf_op jit(solution)/shard_map/ppermute | solution.py:23
  56.0 0.4 level5.1
  56.4 0.1 collective-permute-start.6
  56.5 8.8 %collective-permute-done.6.refs_2_ = s16[328,128]{1,0:T(8,128)(2,1)S(1)} collective-permute-done((s16[328,128]{1,0:T(8,128)(2,1)S(1)}, s16[328,128]{1,0:T(8,128)(2,1)S(1)}, u32[]{:S(2)}, u32[]{:S(2)}) %collective-permute-start.6) | collective-permute-done | bytes 84000 | tf_op jit(solution)/shard_map/ppermute | solution.py:23
  65.3 1.4 %last.1 = f32[512,38]{1,0:T(8,128)} custom-call(s32[5,8,128]{2,1,0:T(8,128)S(1)} %get-tuple-element.27.refs_0_, f32[320,128]{1,0:T(8,128)S(1)} %get-tuple-element.38.refs_1_, s16[328,128]{1,0:T(8,128)(2,1)S(1)} %collective-permute-done.6.refs_2_, bf16[6,38,64,128]{3,2,1,0:T(8,128)(2,1)S(1)} %get-tuple-element.29.refs_2_.refs_3_, ...), custom_call_target="tpu_custom_call" | custom-call | tf_op jit(solution)/shard_map/last/pallas_call | solution.py:328
Async XLA Ops:
  5.5 1.4 %collective-permute-start = (s16[328,128]{1,0:T(8,128)(2,1)S(1)}, s16[328,128]{1,0:T(8,128)(2,1)S(1)}, u32[]{:S(2)}, u32[]{:S(2)}) collective-permute-start(s16[328,128]{1,0:T(8,128)(2,1)S(1)} %get-tuple-element.24), channel_id=1, source_target_pairs={{0,1},{1,0},{2,3},{3,2},{4,5},{5,4},{6,7},{7,6},{8,9},{9,8},{10,11... | collective-permute-start | bytes 251912 | tf_op jit(solution)/shard_map/ppermute | solution.py:23
  7.3 4.7 %collective-permute-start.1 = (s16[328,128]{1,0:T(8,128)(2,1)S(1)}, s16[328,128]{1,0:T(8,128)(2,1)S(1)}, u32[]{:S(2)}, u32[]{:S(2)}) collective-permute-start(s16[328,128]{1,0:T(8,128)(2,1)S(1)} %get-tuple-element.28), channel_id=1, source_target_pairs={{0,2},{2,0},{1,3},{3,1},{4,6},{6,4},{5,7},{7,5},{8,10},{10,8},{9,1... | collective-permute-start | bytes 251912 | tf_op jit(solution)/shard_map/ppermute | solution.py:23
  12.4 6.8 %collective-permute-start.2 = (s16[328,128]{1,0:T(8,128)(2,1)S(1)}, s16[328,128]{1,0:T(8,128)(2,1)S(1)}, u32[]{:S(2)}, u32[]{:S(2)}) collective-permute-start(s16[328,128]{1,0:T(8,128)(2,1)S(1)} %get-tuple-element.31), channel_id=1, source_target_pairs={{0,4},{4,0},{1,5},{5,1},{2,6},{6,2},{3,7},{7,3},{8,12},{12,8},{9,1... | collective-permute-start | bytes 251912 | tf_op jit(solution)/shard_map/ppermute | solution.py:23
  19.5 9.4 %collective-permute-start.3 = (s16[328,128]{1,0:T(8,128)(2,1)S(1)}, s16[328,128]{1,0:T(8,128)(2,1)S(1)}, u32[]{:S(2)}, u32[]{:S(2)}) collective-permute-start(s16[328,128]{1,0:T(8,128)(2,1)S(1)} %get-tuple-element.33), channel_id=1, source_target_pairs={{0,8},{8,0},{1,9},{9,1},{2,10},{10,2},{3,11},{11,3},{4,12},{12,4},... | collective-permute-start | bytes 251912 | tf_op jit(solution)/shard_map/ppermute | solution.py:23
  29.3 20.7 %collective-permute-start.4 = (s16[328,128]{1,0:T(8,128)(2,1)S(1)}, s16[328,128]{1,0:T(8,128)(2,1)S(1)}, u32[]{:S(2)}, u32[]{:S(2)}) collective-permute-start(s16[328,128]{1,0:T(8,128)(2,1)S(1)} %get-tuple-element.35), channel_id=1, source_target_pairs={{0,16},{16,0},{1,17},{17,1},{2,18},{18,2},{3,19},{19,3},{4,20},{20... | collective-permute-start | bytes 251912 | tf_op jit(solution)/shard_map/ppermute | solution.py:23
  50.4 5.5 %collective-permute-start.5 = (s16[328,128]{1,0:T(8,128)(2,1)S(1)}, s16[328,128]{1,0:T(8,128)(2,1)S(1)}, u32[]{:S(2)}, u32[]{:S(2)}) collective-permute-start(s16[328,128]{1,0:T(8,128)(2,1)S(1)} %get-tuple-element.37), channel_id=1, source_target_pairs={{0,32},{32,0},{1,33},{33,1},{2,34},{34,2},{3,35},{35,3},{4,36},{36... | collective-permute-start | bytes 251912 | tf_op jit(solution)/shard_map/ppermute | solution.py:23
  56.4 8.9 %collective-permute-start.6 = (s16[328,128]{1,0:T(8,128)(2,1)S(1)}, s16[328,128]{1,0:T(8,128)(2,1)S(1)}, u32[]{:S(2)}, u32[]{:S(2)}) collective-permute-start(s16[328,128]{1,0:T(8,128)(2,1)S(1)} %get-tuple-element.39), channel_id=1, source_target_pairs={{0,64},{64,0},{1,65},{65,1},{2,66},{66,2},{3,67},{67,3},{4,68},{68... | collective-permute-start | bytes 251912 | tf_op jit(solution)/shard_map/ppermute | solution.py:23

commit v5 on v4

--- a/solution.py
+++ b/solution.py
@@ -11,6 +11,12 @@
 LANES = 128
 BLOCK = 8
 CODE = 32000.0
+SPARE = 6
+FOLD = 16
+
+
+def visit(groups):
+    return [0, groups - 1, *range(1, groups - 1)]
 
 
 def from_partner(block, axis, distance):
@@ -48,18 +54,35 @@
     return high, (value - high.astype(F32)).astype(BF16)
 
 
+def fold(value):
+    free = lanes_of((FOLD, LANES)) % BLOCK >= SPARE
+    rows = [value[row : row + FOLD] for row in range(0, value.shape[0], FOLD)]
+    return jnp.concatenate([jnp.where(free, pltpu.roll(rows[0], BLOCK - 2 * k, 1), rows[k]) for k in range(1, len(rows))], 0)
+
+
+def unfold(value):
+    place = lanes_of((FOLD, LANES)) % BLOCK // 2
+    head = value[:FOLD]
+    for k in range(1, value.shape[0] // FOLD + 1):
+        moved = pltpu.roll(value[(k - 1) * FOLD : k * FOLD], LANES - BLOCK + 2 * k, 1)
+        head = jnp.where(place == k - 1, moved, head)
+    return jnp.concatenate([head, value], 0)
+
+
 def encode(values, send):
-    rank = values[0].shape[0]
+    values = [*values[:-1], fold(values[-1])]
     peak = jnp.full((8, LANES), 1e-30, F32)
     for value in values:
-        for row in range(0, rank, 8):
+        for row in range(0, value.shape[0], 8):
             peak = jnp.maximum(peak, jnp.abs(value[row : row + 8]))
     exponent = jnp.ceil(jnp.log2(peak))
     scale = jnp.exp2(-exponent) * CODE
-    scale = jnp.concatenate([scale] * (rank // 8), 0)
-    for g, value in enumerate(values):
-        send[g * rank : (g + 1) * rank, :] = (value * scale).astype(I32).astype(I16)
-    send[len(values) * rank :, :] = exponent.astype(I32).astype(I16)
+    at = 0
+    for value in values:
+        rows = value.shape[0]
+        send[at : at + rows, :] = (value * jnp.concatenate([scale] * (rows // 8), 0)).astype(I32).astype(I16)
+        at += rows
+    send[at:, :] = exponent.astype(I32).astype(I16)
 
 
 def pick(product, rows, share):
@@ -101,10 +124,13 @@
     first_load.start()
     half = 48
     ids_load.wait()
-    row = lax.broadcasted_iota(I32, (half, LANES), 0)
-    order = jnp.zeros((half, LANES), I32)
-    for o in range(orders):
-        order = jnp.where(row == o, ids[o], order)
+    row = lax.broadcasted_iota(I32, (8, LANES), 0)
+    order = []
+    for begin in range(0, half, 8):
+        order.append(jnp.zeros((8, LANES), I32))
+        for o in range(begin, min(begin + 8, orders)):
+            order[-1] = jnp.where(row == o - begin, ids[o], order[-1])
+    order = jnp.concatenate(order, 0)
     fine_c, fine_s = cos_sin(order * lanes_of((half, LANES)) & nlon - 1, nlon)
     coarse_c, coarse_s = cos_sin(order * (lanes_of((half, LANES)) * LANES) & nlon - 1, nlon)
     turn_c = coarse_c[:, turn // LANES : turn // LANES + 1] + jnp.zeros((half, LANES), F32)
@@ -112,19 +138,19 @@
     for a in range(turn // LANES):
         ca, sa = coarse_c[:, a : a + 1], coarse_s[:, a : a + 1]
         at = slice(a * LANES, (a + 1) * LANES)
-        wave_c[:, at], wave_s[:, at] = ca * fine_c - sa * fine_s, sa * fine_c + ca * fine_s
-
-    def fill(i, carry):
-        for a in range(turn // LANES):
-            at = slice(a * LANES, (a + 1) * LANES)
+        wave_c[:, at], wave_s[:, at] = ca * fine_c - sa * fine_s, -(sa * fine_c + ca * fine_s)
+
+    def fill(a, carry):
+        at = pl.ds(pl.multiple_of(a * LANES, LANES), LANES)
+        c, s = wave_c[:, at], wave_s[:, at]
+        for i in range(nlon // turn):
             to = pl.ds(pl.multiple_of(i * turn + a * LANES, LANES), LANES)
-            c, s = wave_c[:, at], wave_s[:, at]
             table[0:half, to] = c.astype(BF16)
-            table[64 : 64 + half, to] = (-s).astype(BF16)
-            wave_c[:, at], wave_s[:, at] = c * turn_c - s * turn_s, s * turn_c + c * turn_s
+            table[64 : 64 + half, to] = s.astype(BF16)
+            c, s = c * turn_c + s * turn_s, s * turn_c - c * turn_s
         return carry
 
-    lax.fori_loop(0, nlon // turn, fill, 0)
+    lax.fori_loop(0, turn // LANES, fill, 0)
     weights_load.wait()
     leaf_load.wait()
     raw[:, :] = jnp.zeros(raw.shape, F32)
@@ -165,13 +191,16 @@
 
 
 def join(own_ref, got_ref, joined, upper, groups, rank):
-    exponent = got_ref[groups * rank :, :].astype(I32).astype(F32)
+    exponent = got_ref[groups * rank - FOLD :, :].astype(I32).astype(F32)
     scale = jnp.exp2(exponent) * F32(1.0 / CODE)
     scale = jnp.concatenate([scale] * (rank // 8), 0)
-    for g in range(groups):
+    for g in visit(groups):
         at = slice(g * rank, (g + 1) * rank)
         own = own_ref[at, :]
-        other = got_ref[at, :].astype(I32).astype(F32) * scale
+        if g + 1 < groups:
+            other = got_ref[at, :].astype(I32).astype(F32) * scale
+        else:
+            other = unfold(got_ref[g * rank : (g + 1) * rank - FOLD, :].astype(I32).astype(F32) * scale[FOLD:])
         for o, value in enumerate(spread(jnp.where(upper, other, own), 2)):
             joined[g, 2 * o * rank : (2 * o + 1) * rank, :] = value
         for o, value in enumerate(spread(jnp.where(upper, own, other), 2)):
@@ -180,13 +209,13 @@
 
 def merge(factors, joined, groups):
     orders, rank, wide = factors.shape
-    results = []
-    for g in range(groups):
+    results = {}
+    for g in visit(groups):
         first = range(g * BLOCK, min((g + 1) * BLOCK, orders), 2)
         left = jnp.concatenate([jnp.concatenate([factors[o], factors[o + 1]], 1) for o in first], 0)
         product = jnp.dot(left, joined[g], preferred_element_type=F32)
-        results.append(pick(product, rank, 2))
-    return results
+        results[g] = pick(product, rank, 2)
+    return [results[g] for g in range(groups)]
 
 
 def level_kernel(own_ref, got_ref, factors_ref, next_ref, send_ref, joined, *, level):
@@ -273,7 +302,7 @@
     hbm = pl.BlockSpec(memory_space=pltpu.HBM)
     vmem = pl.BlockSpec(memory_space=pltpu.VMEM)
     own_type = pltpu.VMEM((groups * rank, LANES), F32)
-    send_type = pltpu.VMEM((groups * rank + 8, LANES), I16)
+    send_type = pltpu.VMEM((groups * rank - FOLD + 8, LANES), I16)
     joined = pltpu.VMEM((groups, 4 * rank, 2 * LANES), BF16)
     own, send, first = pl.pallas_call(
         lambda *refs: analyse_kernel(*refs, fields=fields, pieces=pieces, turn=1024),

time: 66.8 us -> 66.6 us (level)
  no operation moved by 1% of the time
where the time goes in v5:
time: 66.6 us; the launch traced here: 66.5 us
  starting transfers between devices  29.1 us (44%)
  waiting for transfers between devices  25.6 us (38%)
  Pallas kernels  11.8 us (18%)
    ppermute x7, starting transfers between devices, from_partner(): return lax.ppermute(block, axis, route)  29.1 us
    ppermute x7, waiting for transfers between devices, from_partner(): return lax.ppermute(block, axis, route)  25.6 us
    pallas_call x1, Pallas kernels, body(): pl.pallas_call(lambda *refs: analyse_kernel(*refs, fields=fields, pieces=...  5.55 us
    pallas_call x6, Pallas kernels, body(): pl.pallas_call(lambda *refs, level=level: level_kernel(*refs, level=level...  2.64 us
    pallas_call x1, Pallas kernels, body(): pl.pallas_call(fetch_kernel, out_shape=(pltpu.VMEM((levels - 1,) + transf...  2.23 us
    pallas_call x1, Pallas kernels, body(): pl.pallas_call(lambda *refs: last_kernel(*refs, level=level), out_shape=j...  1.43 us
  transfers between devices with their start and end apart: 7, of which 7 were waited for; matrix products, arithmetic and copies ran while one was open for 0% of the time, Pallas kernels for 3%

profile of v5, /device:TPU:528, one launch (start us, length us, event | category | flops | bytes accessed | tf_op | source)
XLA Modules:
  0.0 66.5 jit_solution(13913288425180019728)
XLA Ops:
  0.0 5.5 %analyse.1 = (f32[320,128]{1,0:T(8,128)S(1)}, s16[312,128]{1,0:T(8,128)(2,1)S(1)}, bf16[38,64,128]{2,1,0:T(8,128)(2,1)S(1)}) custom-call(s32[38]{0:T(128)} %ids_hbm.1, f32[1,64]{1,0:T(1,128)} %bitcast.13, bf16[38,64,64]{2,1,0:T(8,128)(2,1)} %bitcast.11, bf16[7,38,64,128]{3,2,1,0:T(8,128)(2,1)} %bitcast.8, bf16[512,8192]{1,0:T(8,128)(2,1)} %bitcast.10), custom_call_target="tpu_custom_call" | custom-call | tf_op jit(solution)/shard_map/analyse/pallas_call | solution.py:307
  5.6 0.1 collective-permute-start
  5.7 1.2 %collective-permute-done.refs_1_ = s16[312,128]{1,0:T(8,128)(2,1)S(1)} collective-permute-done((s16[312,128]{1,0:T(8,128)(2,1)S(1)}, s16[312,128]{1,0:T(8,128)(2,1)S(1)}, u32[]{:S(2)}, u32[]{:S(2)}) %collective-permute-start) | collective-permute-done | bytes 79904 | tf_op jit(solution)/shard_map/ppermute | solution.py:29
  7.0 0.4 level0.1
  7.4 1.8 %collective-permute-start.1 = (s16[312,128]{1,0:T(8,128)(2,1)S(1)}, s16[312,128]{1,0:T(8,128)(2,1)S(1)}, u32[]{:S(2)}, u32[]{:S(2)}) collective-permute-start(s16[312,128]{1,0:T(8,128)(2,1)S(1)} %get-tuple-element.28), channel_id=1, source_target_pairs={{0,2},{2,0},{1,3},{3,1},{4,6},{6,4},{5,7},{7,5},{8,10},{10,8},{9,1... | collective-permute-start | bytes 239624 | tf_op jit(solution)/shard_map/ppermute | solution.py:29
  9.2 2.2 %fetch.1 = (bf16[6,38,64,128]{3,2,1,0:T(8,128)(2,1)S(1)}, bf16[320,256]{1,0:T(8,128)(2,1)S(1)}, s32[5,8,128]{2,1,0:T(8,128)S(1)}) custom-call(f32[320,128]{1,0:T(8,128)S(1)} %get-tuple-element.26.after_ref.refs_0_, s32[38]{0:T(128)} %ids_hbm.1, bf16[7,38,64,128]{3,2,1,0:T(8,128)(2,1)} %bitcast.9, bf16[38,32,64]{2,1,0:T(8,128)(2,1)} %bitcast.12), custom_call_target="tpu_custom_call" | custom-call | tf_op jit(solution)/shard_map/fetch/pallas_call | solution.py:343
  11.4 0.6 collective-permute-done.1.refs_1_
  12.0 0.4 level1.1
  12.4 2.8 %collective-permute-start.2 = (s16[312,128]{1,0:T(8,128)(2,1)S(1)}, s16[312,128]{1,0:T(8,128)(2,1)S(1)}, u32[]{:S(2)}, u32[]{:S(2)}) collective-permute-start(s16[312,128]{1,0:T(8,128)(2,1)S(1)} %get-tuple-element.31), channel_id=1, source_target_pairs={{0,4},{4,0},{1,5},{5,1},{2,6},{6,2},{3,7},{7,3},{8,12},{12,8},{9,1... | collective-permute-start | bytes 239624 | tf_op jit(solution)/shard_map/ppermute | solution.py:29
  15.3 3.8 %collective-permute-done.2.refs_1_ = s16[312,128]{1,0:T(8,128)(2,1)S(1)} collective-permute-done((s16[312,128]{1,0:T(8,128)(2,1)S(1)}, s16[312,128]{1,0:T(8,128)(2,1)S(1)}, u32[]{:S(2)}, u32[]{:S(2)}) %collective-permute-start.2) | collective-permute-done | bytes 79904 | tf_op jit(solution)/shard_map/ppermute | solution.py:29
  19.1 0.4 level2.1
  19.5 5.9 %collective-permute-start.3 = (s16[312,128]{1,0:T(8,128)(2,1)S(1)}, s16[312,128]{1,0:T(8,128)(2,1)S(1)}, u32[]{:S(2)}, u32[]{:S(2)}) collective-permute-start(s16[312,128]{1,0:T(8,128)(2,1)S(1)} %get-tuple-element.33), channel_id=1, source_target_pairs={{0,8},{8,0},{1,9},{9,1},{2,10},{10,2},{3,11},{11,3},{4,12},{12,4},... | collective-permute-start | bytes 239624 | tf_op jit(solution)/shard_map/ppermute | solution.py:29
  25.4 3.4 %collective-permute-done.3.refs_1_ = s16[312,128]{1,0:T(8,128)(2,1)S(1)} collective-permute-done((s16[312,128]{1,0:T(8,128)(2,1)S(1)}, s16[312,128]{1,0:T(8,128)(2,1)S(1)}, u32[]{:S(2)}, u32[]{:S(2)}) %collective-permute-start.3) | collective-permute-done | bytes 79904 | tf_op jit(solution)/shard_map/ppermute | solution.py:29
  28.8 0.4 level3.1
  29.3 18.2 %collective-permute-start.4 = (s16[312,128]{1,0:T(8,128)(2,1)S(1)}, s16[312,128]{1,0:T(8,128)(2,1)S(1)}, u32[]{:S(2)}, u32[]{:S(2)}) collective-permute-start(s16[312,128]{1,0:T(8,128)(2,1)S(1)} %get-tuple-element.35), channel_id=1, source_target_pairs={{0,16},{16,0},{1,17},{17,1},{2,18},{18,2},{3,19},{19,3},{4,20},{20... | collective-permute-start | bytes 239624 | tf_op jit(solution)/shard_map/ppermute | solution.py:29
  47.4 2.4 %collective-permute-done.4.refs_1_ = s16[312,128]{1,0:T(8,128)(2,1)S(1)} collective-permute-done((s16[312,128]{1,0:T(8,128)(2,1)S(1)}, s16[312,128]{1,0:T(8,128)(2,1)S(1)}, u32[]{:S(2)}, u32[]{:S(2)}) %collective-permute-start.4) | collective-permute-done | bytes 79904 | tf_op jit(solution)/shard_map/ppermute | solution.py:29
  49.9 0.4 level4.1
  50.3 0.1 collective-permute-start.5
  50.4 5.3 %collective-permute-done.5.refs_1_ = s16[312,128]{1,0:T(8,128)(2,1)S(1)} collective-permute-done((s16[312,128]{1,0:T(8,128)(2,1)S(1)}, s16[312,128]{1,0:T(8,128)(2,1)S(1)}, u32[]{:S(2)}, u32[]{:S(2)}) %collective-permute-start.5) | collective-permute-done | bytes 79904 | tf_op jit(solution)/shard_map/ppermute | solution.py:29
  55.8 0.4 level5.1
  56.2 0.1 collective-permute-start.6
  56.4 8.7 %collective-permute-done.6.refs_2_ = s16[312,128]{1,0:T(8,128)(2,1)S(1)} collective-permute-done((s16[312,128]{1,0:T(8,128)(2,1)S(1)}, s16[312,128]{1,0:T(8,128)(2,1)S(1)}, u32[]{:S(2)}, u32[]{:S(2)}) %collective-permute-start.6) | collective-permute-done | bytes 79904 | tf_op jit(solution)/shard_map/ppermute | solution.py:29
  65.1 1.4 %last.1 = f32[512,38]{1,0:T(8,128)} custom-call(s32[5,8,128]{2,1,0:T(8,128)S(1)} %get-tuple-element.27.refs_0_, f32[320,128]{1,0:T(8,128)S(1)} %get-tuple-element.38.refs_1_, s16[312,128]{1,0:T(8,128)(2,1)S(1)} %collective-permute-done.6.refs_2_, bf16[6,38,64,128]{3,2,1,0:T(8,128)(2,1)S(1)} %get-tuple-element.29.refs_2_.refs_3_, ...), custom_call_target="tpu_custom_call" | custom-call | tf_op jit(solution)/shard_map/last/pallas_call | solution.py:357
Async XLA Ops:
  5.6 1.4 %collective-permute-start = (s16[312,128]{1,0:T(8,128)(2,1)S(1)}, s16[312,128]{1,0:T(8,128)(2,1)S(1)}, u32[]{:S(2)}, u32[]{:S(2)}) collective-permute-start(s16[312,128]{1,0:T(8,128)(2,1)S(1)} %get-tuple-element.24), channel_id=1, source_target_pairs={{0,1},{1,0},{2,3},{3,2},{4,5},{5,4},{6,7},{7,6},{8,9},{9,8},{10,11... | collective-permute-start | bytes 239624 | tf_op jit(solution)/shard_map/ppermute | solution.py:29
  7.4 4.6 %collective-permute-start.1 = (s16[312,128]{1,0:T(8,128)(2,1)S(1)}, s16[312,128]{1,0:T(8,128)(2,1)S(1)}, u32[]{:S(2)}, u32[]{:S(2)}) collective-permute-start(s16[312,128]{1,0:T(8,128)(2,1)S(1)} %get-tuple-element.28), channel_id=1, source_target_pairs={{0,2},{2,0},{1,3},{3,1},{4,6},{6,4},{5,7},{7,5},{8,10},{10,8},{9,1... | collective-permute-start | bytes 239624 | tf_op jit(solution)/shard_map/ppermute | solution.py:29
  12.4 6.6 %collective-permute-start.2 = (s16[312,128]{1,0:T(8,128)(2,1)S(1)}, s16[312,128]{1,0:T(8,128)(2,1)S(1)}, u32[]{:S(2)}, u32[]{:S(2)}) collective-permute-start(s16[312,128]{1,0:T(8,128)(2,1)S(1)} %get-tuple-element.31), channel_id=1, source_target_pairs={{0,4},{4,0},{1,5},{5,1},{2,6},{6,2},{3,7},{7,3},{8,12},{12,8},{9,1... | collective-permute-start | bytes 239624 | tf_op jit(solution)/shard_map/ppermute | solution.py:29
  19.5 9.3 %collective-permute-start.3 = (s16[312,128]{1,0:T(8,128)(2,1)S(1)}, s16[312,128]{1,0:T(8,128)(2,1)S(1)}, u32[]{:S(2)}, u32[]{:S(2)}) collective-permute-start(s16[312,128]{1,0:T(8,128)(2,1)S(1)} %get-tuple-element.33), channel_id=1, source_target_pairs={{0,8},{8,0},{1,9},{9,1},{2,10},{10,2},{3,11},{11,3},{4,12},{12,4},... | collective-permute-start | bytes 239624 | tf_op jit(solution)/shard_map/ppermute | solution.py:29
  29.3 20.6 %collective-permute-start.4 = (s16[312,128]{1,0:T(8,128)(2,1)S(1)}, s16[312,128]{1,0:T(8,128)(2,1)S(1)}, u32[]{:S(2)}, u32[]{:S(2)}) collective-permute-start(s16[312,128]{1,0:T(8,128)(2,1)S(1)} %get-tuple-element.35), channel_id=1, source_target_pairs={{0,16},{16,0},{1,17},{17,1},{2,18},{18,2},{3,19},{19,3},{4,20},{20... | collective-permute-start | bytes 239624 | tf_op jit(solution)/shard_map/ppermute | solution.py:29
  50.3 5.5 %collective-permute-start.5 = (s16[312,128]{1,0:T(8,128)(2,1)S(1)}, s16[312,128]{1,0:T(8,128)(2,1)S(1)}, u32[]{:S(2)}, u32[]{:S(2)}) collective-permute-start(s16[312,128]{1,0:T(8,128)(2,1)S(1)} %get-tuple-element.37), channel_id=1, source_target_pairs={{0,32},{32,0},{1,33},{33,1},{2,34},{34,2},{3,35},{35,3},{4,36},{36... | collective-permute-start | bytes 239624 | tf_op jit(solution)/shard_map/ppermute | solution.py:29
  56.2 8.9 %collective-permute-start.6 = (s16[312,128]{1,0:T(8,128)(2,1)S(1)}, s16[312,128]{1,0:T(8,128)(2,1)S(1)}, u32[]{:S(2)}, u32[]{:S(2)}) collective-permute-start(s16[312,128]{1,0:T(8,128)(2,1)S(1)} %get-tuple-element.39), channel_id=1, source_target_pairs={{0,64},{64,0},{1,65},{65,1},{2,66},{66,2},{3,67},{67,3},{4,68},{68... | collective-permute-start | bytes 239624 | tf_op jit(solution)/shard_map/ppermute | solution.py:29

commit v6 on v5

--- a/solution.py
+++ b/solution.py
@@ -16,7 +16,7 @@
 
 
 def visit(groups):
-    return [0, groups - 1, *range(1, groups - 1)]
+    return [0, 1, groups - 1, *range(2, groups - 1)]
 
 
 def from_partner(block, axis, distance):

time: 66.6 us -> 66.4 us (level)
  waiting for transfers between devices: 25.6 us -> 24.6 us
  starting transfers between devices: 29.1 us -> 30 us
    ppermute x7, waiting for transfers between devices: 25.6 us -> 24.6 us  [from_partner(): return lax.ppermute(block, axis, route)]
    ppermute x7, starting transfers between devices: 29.1 us -> 30 us  [from_partner(): return lax.ppermute(block, axis, route)]
where the time goes in v6:
time: 66.4 us; the launch traced here: 66.3 us
  starting transfers between devices  30 us (45%)
  waiting for transfers between devices  24.6 us (37%)
  Pallas kernels  11.6 us (17%)
    ppermute x7, starting transfers between devices, from_partner(): return lax.ppermute(block, axis, route)  30 us
    ppermute x7, waiting for transfers between devices, from_partner(): return lax.ppermute(block, axis, route)  24.6 us
    pallas_call x1, Pallas kernels, body(): pl.pallas_call(lambda *refs: analyse_kernel(*refs, fields=fields, pieces=...  5.55 us
    pallas_call x6, Pallas kernels, body(): pl.pallas_call(lambda *refs, level=level: level_kernel(*refs, level=level...  2.48 us
    pallas_call x1, Pallas kernels, body(): pl.pallas_call(fetch_kernel, out_shape=(pltpu.VMEM((levels - 1,) + transf...  2.23 us
    pallas_call x1, Pallas kernels, body(): pl.pallas_call(lambda *refs: last_kernel(*refs, level=level), out_shape=j...  1.39 us
  transfers between devices with their start and end apart: 7, of which 7 were waited for; matrix products, arithmetic and copies ran while one was open for 0% of the time, Pallas kernels for 3%

profile of v6, /device:TPU:528, one launch (start us, length us, event | category | flops | bytes accessed | tf_op | source)
XLA Modules:
  0.0 66.3 jit_solution(18295227835548527362)
XLA Ops:
  0.0 5.5 %analyse.1 = (f32[320,128]{1,0:T(8,128)S(1)}, s16[312,128]{1,0:T(8,128)(2,1)S(1)}, bf16[38,64,128]{2,1,0:T(8,128)(2,1)S(1)}) custom-call(s32[38]{0:T(128)} %ids_hbm.1, f32[1,64]{1,0:T(1,128)} %bitcast.13, bf16[38,64,64]{2,1,0:T(8,128)(2,1)} %bitcast.11, bf16[7,38,64,128]{3,2,1,0:T(8,128)(2,1)} %bitcast.8, bf16[512,8192]{1,0:T(8,128)(2,1)} %bitcast.10), custom_call_target="tpu_custom_call" | custom-call | tf_op jit(solution)/shard_map/analyse/pallas_call | solution.py:307
  5.6 0.1 collective-permute-start
  5.7 1.2 %collective-permute-done.refs_1_ = s16[312,128]{1,0:T(8,128)(2,1)S(1)} collective-permute-done((s16[312,128]{1,0:T(8,128)(2,1)S(1)}, s16[312,128]{1,0:T(8,128)(2,1)S(1)}, u32[]{:S(2)}, u32[]{:S(2)}) %collective-permute-start) | collective-permute-done | bytes 79904 | tf_op jit(solution)/shard_map/ppermute | solution.py:29
  7.0 0.4 level0.1
  7.4 1.8 %collective-permute-start.1 = (s16[312,128]{1,0:T(8,128)(2,1)S(1)}, s16[312,128]{1,0:T(8,128)(2,1)S(1)}, u32[]{:S(2)}, u32[]{:S(2)}) collective-permute-start(s16[312,128]{1,0:T(8,128)(2,1)S(1)} %get-tuple-element.28), channel_id=1, source_target_pairs={{0,2},{2,0},{1,3},{3,1},{4,6},{6,4},{5,7},{7,5},{8,10},{10,8},{9,1... | collective-permute-start | bytes 239624 | tf_op jit(solution)/shard_map/ppermute | solution.py:29
  9.1 2.2 %fetch.1 = (bf16[6,38,64,128]{3,2,1,0:T(8,128)(2,1)S(1)}, bf16[320,256]{1,0:T(8,128)(2,1)S(1)}, s32[5,8,128]{2,1,0:T(8,128)S(1)}) custom-call(f32[320,128]{1,0:T(8,128)S(1)} %get-tuple-element.26.after_ref.refs_0_, s32[38]{0:T(128)} %ids_hbm.1, bf16[7,38,64,128]{3,2,1,0:T(8,128)(2,1)} %bitcast.9, bf16[38,32,64]{2,1,0:T(8,128)(2,1)} %bitcast.12), custom_call_target="tpu_custom_call" | custom-call | tf_op jit(solution)/shard_map/fetch/pallas_call | solution.py:343
  11.4 0.6 collective-permute-done.1.refs_1_
  12.0 0.4 level1.1
  12.4 2.8 %collective-permute-start.2 = (s16[312,128]{1,0:T(8,128)(2,1)S(1)}, s16[312,128]{1,0:T(8,128)(2,1)S(1)}, u32[]{:S(2)}, u32[]{:S(2)}) collective-permute-start(s16[312,128]{1,0:T(8,128)(2,1)S(1)} %get-tuple-element.31), channel_id=1, source_target_pairs={{0,4},{4,0},{1,5},{5,1},{2,6},{6,2},{3,7},{7,3},{8,12},{12,8},{9,1... | collective-permute-start | bytes 239624 | tf_op jit(solution)/shard_map/ppermute | solution.py:29
  15.2 3.0 %collective-permute-done.2.refs_1_ = s16[312,128]{1,0:T(8,128)(2,1)S(1)} collective-permute-done((s16[312,128]{1,0:T(8,128)(2,1)S(1)}, s16[312,128]{1,0:T(8,128)(2,1)S(1)}, u32[]{:S(2)}, u32[]{:S(2)}) %collective-permute-start.2) | collective-permute-done | bytes 79904 | tf_op jit(solution)/shard_map/ppermute | solution.py:29
  18.1 0.4 level2.1
  18.6 6.7 %collective-permute-start.3 = (s16[312,128]{1,0:T(8,128)(2,1)S(1)}, s16[312,128]{1,0:T(8,128)(2,1)S(1)}, u32[]{:S(2)}, u32[]{:S(2)}) collective-permute-start(s16[312,128]{1,0:T(8,128)(2,1)S(1)} %get-tuple-element.33), channel_id=1, source_target_pairs={{0,8},{8,0},{1,9},{9,1},{2,10},{10,2},{3,11},{11,3},{4,12},{12,4},... | collective-permute-start | bytes 239624 | tf_op jit(solution)/shard_map/ppermute | solution.py:29
  25.3 3.3 %collective-permute-done.3.refs_1_ = s16[312,128]{1,0:T(8,128)(2,1)S(1)} collective-permute-done((s16[312,128]{1,0:T(8,128)(2,1)S(1)}, s16[312,128]{1,0:T(8,128)(2,1)S(1)}, u32[]{:S(2)}, u32[]{:S(2)}) %collective-permute-start.3) | collective-permute-done | bytes 79904 | tf_op jit(solution)/shard_map/ppermute | solution.py:29
  28.6 0.4 level3.1
  29.0 18.3 %collective-permute-start.4 = (s16[312,128]{1,0:T(8,128)(2,1)S(1)}, s16[312,128]{1,0:T(8,128)(2,1)S(1)}, u32[]{:S(2)}, u32[]{:S(2)}) collective-permute-start(s16[312,128]{1,0:T(8,128)(2,1)S(1)} %get-tuple-element.35), channel_id=1, source_target_pairs={{0,16},{16,0},{1,17},{17,1},{2,18},{18,2},{3,19},{19,3},{4,20},{20... | collective-permute-start | bytes 239624 | tf_op jit(solution)/shard_map/ppermute | solution.py:29
  47.3 2.4 %collective-permute-done.4.refs_1_ = s16[312,128]{1,0:T(8,128)(2,1)S(1)} collective-permute-done((s16[312,128]{1,0:T(8,128)(2,1)S(1)}, s16[312,128]{1,0:T(8,128)(2,1)S(1)}, u32[]{:S(2)}, u32[]{:S(2)}) %collective-permute-start.4) | collective-permute-done | bytes 79904 | tf_op jit(solution)/shard_map/ppermute | solution.py:29
  49.7 0.4 level4.1
  50.2 0.1 collective-permute-start.5
  50.3 5.3 %collective-permute-done.5.refs_1_ = s16[312,128]{1,0:T(8,128)(2,1)S(1)} collective-permute-done((s16[312,128]{1,0:T(8,128)(2,1)S(1)}, s16[312,128]{1,0:T(8,128)(2,1)S(1)}, u32[]{:S(2)}, u32[]{:S(2)}) %collective-permute-start.5) | collective-permute-done | bytes 79904 | tf_op jit(solution)/shard_map/ppermute | solution.py:29
  55.6 0.4 level5.1
  56.0 0.1 collective-permute-start.6
  56.2 8.7 %collective-permute-done.6.refs_2_ = s16[312,128]{1,0:T(8,128)(2,1)S(1)} collective-permute-done((s16[312,128]{1,0:T(8,128)(2,1)S(1)}, s16[312,128]{1,0:T(8,128)(2,1)S(1)}, u32[]{:S(2)}, u32[]{:S(2)}) %collective-permute-start.6) | collective-permute-done | bytes 79904 | tf_op jit(solution)/shard_map/ppermute | solution.py:29
  64.9 1.4 %last.1 = f32[512,38]{1,0:T(8,128)} custom-call(s32[5,8,128]{2,1,0:T(8,128)S(1)} %get-tuple-element.27.refs_0_, f32[320,128]{1,0:T(8,128)S(1)} %get-tuple-element.38.refs_1_, s16[312,128]{1,0:T(8,128)(2,1)S(1)} %collective-permute-done.6.refs_2_, bf16[6,38,64,128]{3,2,1,0:T(8,128)(2,1)S(1)} %get-tuple-element.29.refs_2_.refs_3_, ...), custom_call_target="tpu_custom_call" | custom-call | tf_op jit(solution)/shard_map/last/pallas_call | solution.py:357
Async XLA Ops:
  5.6 1.4 %collective-permute-start = (s16[312,128]{1,0:T(8,128)(2,1)S(1)}, s16[312,128]{1,0:T(8,128)(2,1)S(1)}, u32[]{:S(2)}, u32[]{:S(2)}) collective-permute-start(s16[312,128]{1,0:T(8,128)(2,1)S(1)} %get-tuple-element.24), channel_id=1, source_target_pairs={{0,1},{1,0},{2,3},{3,2},{4,5},{5,4},{6,7},{7,6},{8,9},{9,8},{10,11... | collective-permute-start | bytes 239624 | tf_op jit(solution)/shard_map/ppermute | solution.py:29
  7.4 4.6 %collective-permute-start.1 = (s16[312,128]{1,0:T(8,128)(2,1)S(1)}, s16[312,128]{1,0:T(8,128)(2,1)S(1)}, u32[]{:S(2)}, u32[]{:S(2)}) collective-permute-start(s16[312,128]{1,0:T(8,128)(2,1)S(1)} %get-tuple-element.28), channel_id=1, source_target_pairs={{0,2},{2,0},{1,3},{3,1},{4,6},{6,4},{5,7},{7,5},{8,10},{10,8},{9,1... | collective-permute-start | bytes 239624 | tf_op jit(solution)/shard_map/ppermute | solution.py:29
  12.4 5.8 %collective-permute-start.2 = (s16[312,128]{1,0:T(8,128)(2,1)S(1)}, s16[312,128]{1,0:T(8,128)(2,1)S(1)}, u32[]{:S(2)}, u32[]{:S(2)}) collective-permute-start(s16[312,128]{1,0:T(8,128)(2,1)S(1)} %get-tuple-element.31), channel_id=1, source_target_pairs={{0,4},{4,0},{1,5},{5,1},{2,6},{6,2},{3,7},{7,3},{8,12},{12,8},{9,1... | collective-permute-start | bytes 239624 | tf_op jit(solution)/shard_map/ppermute | solution.py:29
  18.6 10.0 %collective-permute-start.3 = (s16[312,128]{1,0:T(8,128)(2,1)S(1)}, s16[312,128]{1,0:T(8,128)(2,1)S(1)}, u32[]{:S(2)}, u32[]{:S(2)}) collective-permute-start(s16[312,128]{1,0:T(8,128)(2,1)S(1)} %get-tuple-element.33), channel_id=1, source_target_pairs={{0,8},{8,0},{1,9},{9,1},{2,10},{10,2},{3,11},{11,3},{4,12},{12,4},... | collective-permute-start | bytes 239624 | tf_op jit(solution)/shard_map/ppermute | solution.py:29
  29.0 20.7 %collective-permute-start.4 = (s16[312,128]{1,0:T(8,128)(2,1)S(1)}, s16[312,128]{1,0:T(8,128)(2,1)S(1)}, u32[]{:S(2)}, u32[]{:S(2)}) collective-permute-start(s16[312,128]{1,0:T(8,128)(2,1)S(1)} %get-tuple-element.35), channel_id=1, source_target_pairs={{0,16},{16,0},{1,17},{17,1},{2,18},{18,2},{3,19},{19,3},{4,20},{20... | collective-permute-start | bytes 239624 | tf_op jit(solution)/shard_map/ppermute | solution.py:29
  50.2 5.5 %collective-permute-start.5 = (s16[312,128]{1,0:T(8,128)(2,1)S(1)}, s16[312,128]{1,0:T(8,128)(2,1)S(1)}, u32[]{:S(2)}, u32[]{:S(2)}) collective-permute-start(s16[312,128]{1,0:T(8,128)(2,1)S(1)} %get-tuple-element.37), channel_id=1, source_target_pairs={{0,32},{32,0},{1,33},{33,1},{2,34},{34,2},{3,35},{35,3},{4,36},{36... | collective-permute-start | bytes 239624 | tf_op jit(solution)/shard_map/ppermute | solution.py:29
  56.0 8.9 %collective-permute-start.6 = (s16[312,128]{1,0:T(8,128)(2,1)S(1)}, s16[312,128]{1,0:T(8,128)(2,1)S(1)}, u32[]{:S(2)}, u32[]{:S(2)}) collective-permute-start(s16[312,128]{1,0:T(8,128)(2,1)S(1)} %get-tuple-element.39), channel_id=1, source_target_pairs={{0,64},{64,0},{1,65},{65,1},{2,66},{66,2},{3,67},{67,3},{4,68},{68... | collective-permute-start | bytes 239624 | tf_op jit(solution)/shard_map/ppermute | solution.py:29
